TPU v7x, 32 devices: a whole 2x2x4 slice. The times are simulated.
32 devices in a mesh: gx: 4 (over x, core), gy: 2 (over y), gz: 4 (over z).
Axes of the slice: x: 2, y: 2, z: 4, core: 2. Of those that a mesh axis runs over, the one named last changes fastest.
Arguments:
- head_inputs: bfloat16 [8192, 2048], P(('gx', 'gy', 'gz')), may hold values from -6 to 6
- step_raw: float32 [8192, 32], P(('gx', 'gy', 'gz')), may hold values from -4 to 4
- state_in: bfloat16 [8192, 128], P(('gx', 'gy', 'gz')), may hold values from -0.119628906 to 0.119628906
- state_out: bfloat16 [8192, 128], P(('gx', 'gy', 'gz')), may hold values from -0.119628906 to 0.119628906
- decay_log: float32 [32], replicated, may hold values from -13.5 to -3
- step_bias: float32 [32], replicated, may hold values from -1 to 0.5
- skip_gain: float32 [32], replicated, may hold values from 0.5 to 1.5
- checkpoints: bfloat16 [32, 32, 64, 128], P(('gx', 'gy'), None, 'gz'), may hold values from -6 to 6
- out_grad: bfloat16 [8192, 2048], P(('gx', 'gy', 'gz')), may hold values from -6 to 6
Outputs:
- input_grad: bfloat16 [8192, 2048], P(('gx', 'gy', 'gz'))
- step_grad: float32 [8192, 32], P(('gx', 'gy', 'gz'))
- state_in_grad: float32 [8192, 128], P(('gx', 'gy', 'gz'))
- state_out_grad: float32 [8192, 128], P(('gx', 'gy', 'gz'))
- decay_log_grad: float32 [32], replicated
- step_bias_grad: float32 [32], replicated
- skip_gain_grad: float32 [32], replicated
All inputs are finite; a program needn't handle non-finite values.
Results may differ from a plain program's by a relative error of at most 0.00065.
Values may be sent and summed in bfloat16 or wider, within the bound.
A program may use at most 128 MiB of HBM per device.

v0:
```python
import jax
import jax.numpy as jnp
from jax import lax
from jax.sharding import PartitionSpec as P

highest = lax.Precision.HIGHEST


def carried_in(array, axis, combine, identity):
    length, index = (lax.axis_size(axis), lax.axis_index(axis))
    everything = jax.tree.map(lambda part: lax.all_gather(part, axis), array)
    start = jax.tree.map(
        lambda part, zero: jnp.broadcast_to(jnp.asarray(zero, part.dtype), part.shape),
        array,
        identity,
    )

    def hop(k, before):
        at = length - 1 - k
        reached = at > index
        new = combine(before, jax.tree.map(lambda part: part[at], everything))
        return jax.tree.map(lambda a, b: jnp.where(reached, a, b), new, before)

    return lax.fori_loop(0, length, hop, start)


def block_forward(inputs, raw, b_mat, scores, read, decay_log, bias, skip, start):
    step = jax.nn.softplus(raw + bias)
    cum = jnp.cumsum(step * -jnp.exp(decay_log), axis=0)
    length = inputs.shape[0]
    rows = lax.broadcasted_iota(jnp.int32, (length, length), 0)
    cols = lax.broadcasted_iota(jnp.int32, (length, length), 1)
    lower = rows >= cols
    ctrans = cum.T
    gap = ctrans[:, :, None] - ctrans[:, None, :]
    mix = jnp.where(lower, jnp.exp(jnp.where(lower, gap, 0.0)), 0.0) * scores * step.T[:, None, :]
    inner = jnp.einsum("hts,shp->thp", mix, inputs, precision=highest)
    carried = read * jnp.exp(cum)[:, :, None]
    result = inner + carried + skip[None, :, None] * inputs
    tail = jnp.exp(cum[-1][None, :] - cum) * step
    final = jnp.exp(cum[-1])[:, None, None] * start + jnp.einsum(
        "sh,shp,sn->hpn", tail, inputs, b_mat, precision=highest
    )
    return (result, final)


def span_forward(inputs, raw, b_mat, scores, read, decay_log, bias, skip, start):
    length, heads = raw.shape
    width = inputs.shape[1] // heads
    states = start.shape[2]
    block = min(8, heads)
    blocks = heads // block
    grouped = inputs.reshape(length, blocks, block, width).transpose(1, 0, 2, 3)
    read_g = read.reshape(length, blocks, block, width).transpose(1, 0, 2, 3)
    raw_g = raw.reshape(length, blocks, block).transpose(1, 0, 2)

    def one_block(items):
        return block_forward(
            items[0], items[1], b_mat, scores, items[2], items[3], items[4], items[5], items[6]
        )

    result, final = lax.map(
        one_block,
        (
            grouped,
            raw_g,
            read_g,
            decay_log.reshape(blocks, block),
            bias.reshape(blocks, block),
            skip.reshape(blocks, block),
            start.reshape(blocks, block, width, states),
        ),
    )
    result = result.transpose(1, 0, 2, 3).reshape(length, heads * width)
    return (result, final.reshape(heads, width, states))


def combine(earlier, later):
    return (earlier[0] * later[0], later[0][:, None, None] * earlier[1] + later[1])


def local(
    head_inputs,
    step_raw,
    state_in,
    state_out,
    decay_log,
    step_bias,
    skip_gain,
    checkpoints,
    out_grad,
):
    entering = lax.all_to_all(checkpoints, "gz", split_axis=0, concat_axis=2, tiled=True)[0]
    start = entering.astype(jnp.float32)
    length, heads = step_raw.shape
    width = head_inputs.shape[1] // heads
    states = state_in.shape[1]
    c_mat = state_out.astype(jnp.float32)
    b_mat = state_in.astype(jnp.float32)
    grad_rows = out_grad.astype(jnp.float32)
    step = jax.nn.softplus(step_raw + step_bias)
    cum = jnp.cumsum(step * -jnp.exp(decay_log), axis=0)
    weighted = (grad_rows.reshape(length, heads, width) * jnp.exp(cum)[:, :, None]).reshape(
        length, heads * width
    )
    local_term = jnp.dot(weighted.T, c_mat, precision=highest).reshape(heads, width, states)
    decays = jnp.exp(cum[-1])
    group = lax.axis_size("gz")
    spread = jnp.broadcast_to(decays[None, :, None], (1, heads, group))
    got_decay, got_term = (
        lax.all_to_all(spread, "gz", split_axis=2, concat_axis=0, tiled=True),
        lax.all_to_all(local_term[None], "gz", split_axis=2, concat_axis=0, tiled=True),
    )
    got_decay = got_decay[:, :, 0]
    slice_width = got_term.shape[2]
    suffix_b = jnp.zeros((heads, slice_width, states), jnp.float32)
    suffix_a = jnp.ones((heads,), jnp.float32)
    inners = [None] * group
    leads = [None] * group
    for member in reversed(range(group)):
        inners[member] = suffix_b
        leads[member] = suffix_a
        suffix_b = got_term[member] + got_decay[member][:, None, None] * suffix_b
        suffix_a = got_decay[member] * suffix_a
    total = (suffix_a, suffix_b)
    neutral = (
        jnp.ones((heads,), jnp.float32),
        jnp.zeros((heads, slice_width, states), jnp.float32),
    )
    outer = carried_in(total, ("gx", "gy"), combine, neutral)
    carries = jnp.stack(
        [inners[member] + leads[member][:, None, None] * outer[1] for member in range(group)]
    )
    later = lax.all_to_all(carries, "gz", split_axis=0, concat_axis=2, tiled=True)[0]
    flat_start = entering.reshape(heads * width, states)
    scores = jnp.dot(state_out, state_in.T, preferred_element_type=jnp.float32)
    read = jnp.dot(state_out, flat_start.T, preferred_element_type=jnp.float32)
    _, pull = jax.vjp(
        span_forward,
        head_inputs.astype(jnp.float32),
        step_raw,
        b_mat,
        scores,
        read,
        decay_log,
        step_bias,
        skip_gain,
        start,
    )
    grads = pull((grad_rows, later))
    b_grad = grads[2] + jnp.dot(grads[3].T, c_mat, precision=highest)
    c_grad = jnp.dot(grads[3], b_mat, precision=highest) + jnp.dot(
        grads[4], flat_start.astype(jnp.float32), precision=highest
    )
    decay_sum, bias_sum, skip_sum = lax.psum((grads[5], grads[6], grads[7]), ("gx", "gy", "gz"))
    return (grads[0].astype(jnp.bfloat16), grads[1], b_grad, c_grad, decay_sum, bias_sum, skip_sum)


def solution(mesh):
    placed = (
        P(("gx", "gy", "gz"), None),
        P(("gx", "gy", "gz"), None),
        P(("gx", "gy", "gz"), None),
        P(("gx", "gy", "gz"), None),
        P(),
        P(),
        P(),
        P(("gx", "gy"), None, "gz", None),
        P(("gx", "gy", "gz"), None),
    )
    return jax.shard_map(
        local,
        mesh=mesh,
        in_specs=placed,
        out_specs=(
            P(("gx", "gy", "gz"), None),
            P(("gx", "gy", "gz"), None),
            P(("gx", "gy", "gz"), None),
            P(("gx", "gy", "gz"), None),
            P(),
            P(),
            P(),
        ),
        check_vma=False,
    )
```

profile of v0, /device:TPU:0, one launch (start us, length us, event | category | flops | bytes accessed | tf_op | source)
XLA Modules:
  0.0 378.9 jit_solution(17736922358008201280)
XLA Ops:
  10.4 6.3 %all-to-all-start.1 = ((f32[1,32,4]{1,0,2:T(1,128)}), f32[1,32,4]{1,0,2:T(1,128)S(1)}, u32[]{:S(2)}, u32[]{:S(2)}) async-start(f32[1,32,4]{1,0,2:T(1,128)} %broadcast_in_dim.201), calls=%async_computation.1 | async-start | bytes 4096 | tf_op jit(solution)/shard_map/all_to_all | solution.py:111
  22.2 4.0 %all-to-all-start = ((f32[1,32,64,128]{3,1,0,2:T(8,128)}), f32[1,32,64,128]{3,1,0,2:T(8,128)S(1)}, u32[]{:S(2)}, u32[]{:S(2)}) async-start(f32[1,32,64,128]{3,1,0,2:T(8,128)} %copy.131), calls=%async_computation | async-start | bytes 2097152 | tf_op jit(solution)/shard_map/all_to_all | solution.py:112
  27.3 24.1 %all-to-all-done = f32[1,32,64,128]{3,1,0,2:T(8,128)S(1)} async-done(((f32[1,32,64,128]{3,1,0,2:T(8,128)}), f32[1,32,64,128]{3,1,0,2:T(8,128)S(1)}, u32[]{:S(2)}, u32[]{:S(2)}) %all-to-all-start) | async-done | bytes 1048608 | tf_op jit(solution)/shard_map/all_to_all | solution.py:112
  53.0 3.6 all-to-all-start.3
  59.8 12.3 %all-gather = f32[8,1,32,1]{2,3,1,0:T(1,128)S(1)} all-gather(f32[1,1,32,1]{2,3,1,0:T(1,128)S(1)} %get-tuple-element.2007), channel_id=2, replica_groups=mesh['gx'=4,'gy'=2,'gz'=4] {'gx','gy'}, dimensions={0}, use_global_device_ids=true | all-gather | bytes 1152 | tf_op jit(solution)/shard_map/all_gather | solution.py:11
  72.1 7.9 %all-gather.3.cloned.1.call-done = f32[8,32,16,128]{3,2,1,0:T(8,128)} async-done(((f32[1,32,16,128]{3,2,1,0:T(8,128)}), f32[8,32,16,128]{3,2,1,0:T(8,128)}) %all-gather.3.cloned.1.call-update) | async-done | bytes 2097168 | tf_op jit(solution)/shard_map/all_gather | solution.py:11
  80.0 9.1 %while.92 = (s32[]{:T(128)}, f32[32,16,128]{2,1,0:T(8,128)S(1)}, s32[]{:T(128)}, f32[8,32]{1,0:T(8,128)S(1)}, f32[8,32,16,128]{3,2,1,0:T(8,128)}, /*index=5*/s32[]{:T(128)}, s32[]{:T(128)}, s32[]{:T(128)}, s32[]{:T(128)}) while((s32[]{:T(128)}, f32[32,16,128]{2,1,0:T(8,128)S(1)}, s32[]{:T(128)}, f32[8,32]{1,0:T(8,128)S(1)}, ...), condition=%wide.region_3.4_spmd.clone, body=%wide.region_2.3_spmd.clone.sunk | while | flops 262152 | bytes 786983 | solution.py:24
  90.5 4.7 %all-to-all-start.2 = ((f32[4,32,16,128]{3,2,1,0:T(8,128)}), f32[4,32,16,128]{3,2,1,0:T(8,128)}, u32[]{:S(2)}, u32[]{:S(2)}) async-start(f32[4,32,16,128]{3,2,1,0:T(8,128)} %pad_maximum_fusion), calls=%async_computation.2 | async-start | bytes 2097152 | tf_op jit(solution)/shard_map/all_to_all | solution.py:134
  100.4 51.9 %while.91 = (s32[]{:T(128)}, f32[4,256,8]{1,2,0:T(8,128)}, f32[4,8]{1,0:T(4,128)}, f32[4,1,8]{2,1,0:T(1,128)}, f32[4,256,8]{1,2,0:T(8,128)}, /*index=5*/f32[4,8,...) while((s32[]{:T(128)}, f32[4,256,8]{1,2,0:T(8,128)}, ...), condition=%wide.region_7.8_spmd.clone.clone, body=%wide.region_4.7_spmd.clone.clone.sunk | while | flops 3090474 | bytes 14179661 | solution.py:62
  101.4 4.2 %multiply_dynamic-update-slice_fusion.4 = (f32[4,8,256,256]{3,2,1,0:T(8,128)}, f32[4,8,256,256]{3,2,1,0:T(8,128)}, f32[4,8,256,256]{3,2,1,0:T(8,128)}, f32[4,8,256,256]{3,2,1,0:T(8,128)}) fusion(f32[4,8,256,256]{3,2,1,0:T(8,128)} %get-tuple-element.2479, s32[]{:T(128)} %get-tuple-element.2470, f32[8,256]{1,0:T(8,128)S(1)} %get-tuple-element.2383, ...), kind=kLoop, calls=%fused_computation.5.clone.1 | loop fusion | flops 2621440 | bytes 8741376 | tf_op jit(solution)/shard_map/jvp()/while/body/jit(dynamic_update_index_in_dim)/dynamic_update_slice | solution.py:62
  114.5 4.0 %multiply_dynamic-update-slice_fusion.4 = (f32[4,8,256,256]{3,2,1,0:T(8,128)}, f32[4,8,256,256]{3,2,1,0:T(8,128)}, f32[4,8,256,256]{3,2,1,0:T(8,128)}, f32[4,8,256,256]{3,2,1,0:T(8,128)}) fusion(f32[4,8,256,256]{3,2,1,0:T(8,128)} %get-tuple-element.2479, s32[]{:T(128)} %get-tuple-element.2470, f32[8,256]{1,0:T(8,128)S(1)} %get-tuple-element.2383, ...), kind=kLoop, calls=%fused_computation.5.clone.1 | loop fusion | flops 2621440 | bytes 8741376 | tf_op jit(solution)/shard_map/jvp()/while/body/jit(dynamic_update_index_in_dim)/dynamic_update_slice | solution.py:62
  127.4 4.2 %multiply_dynamic-update-slice_fusion.4 = (f32[4,8,256,256]{3,2,1,0:T(8,128)}, f32[4,8,256,256]{3,2,1,0:T(8,128)}, f32[4,8,256,256]{3,2,1,0:T(8,128)}, f32[4,8,256,256]{3,2,1,0:T(8,128)}) fusion(f32[4,8,256,256]{3,2,1,0:T(8,128)} %get-tuple-element.2479, s32[]{:T(128)} %get-tuple-element.2470, f32[8,256]{1,0:T(8,128)S(1)} %get-tuple-element.2383, ...), kind=kLoop, calls=%fused_computation.5.clone.1 | loop fusion | flops 2621440 | bytes 8741376 | tf_op jit(solution)/shard_map/jvp()/while/body/jit(dynamic_update_index_in_dim)/dynamic_update_slice | solution.py:62
  140.4 4.0 %multiply_dynamic-update-slice_fusion.4 = (f32[4,8,256,256]{3,2,1,0:T(8,128)}, f32[4,8,256,256]{3,2,1,0:T(8,128)}, f32[4,8,256,256]{3,2,1,0:T(8,128)}, f32[4,8,256,256]{3,2,1,0:T(8,128)}) fusion(f32[4,8,256,256]{3,2,1,0:T(8,128)} %get-tuple-element.2479, s32[]{:T(128)} %get-tuple-element.2470, f32[8,256]{1,0:T(8,128)S(1)} %get-tuple-element.2383, ...), kind=kLoop, calls=%fused_computation.5.clone.1 | loop fusion | flops 2621440 | bytes 8741376 | tf_op jit(solution)/shard_map/jvp()/while/body/jit(dynamic_update_index_in_dim)/dynamic_update_slice | solution.py:62
  164.9 157.2 %while.93 = (s32[]{:T(128)}, f32[256,256]{1,0:T(8,128)S(1)}, f32[256,128]{1,0:T(8,128)}, bf16[4,256,8,64]{1,3,2,0:T(8,128)(2,1)}, f32[4,256,8]{1,2,0:T(8,128)}, ...) while((s32[]{:T(128)}, f32[256,256]{1,0:T(8,128)S(1)}, ...), condition=%wide.region_21.22_spmd.clone.clone, body=%wide.region_8.21_spmd.clone.clone.sunk | while | flops 1215725568 | bytes 18326480 | solution.py:62
  170.2 6.5 %fusion.136 = (f32[8,256]{1,0:T(8,128)}, f32[8,256]{1,0:T(8,128)}, f32[256,256]{1,0:T(8,128)S(1)}, f32[8,256]{1,0:T(8,128)}) fusion(f32[4,8,256,256]{3,2,1,0:T(8,128)} %get-tuple-element.2652, s32[]{:T(128)S(6)} %sub.159, f32[256,256]{1,0:T(8,128)S(1)} %bitcast.499, f32[8,256]{1,0:T(8,128)S(1)} %dynamic-slice_bitcast_fusion.9, ...), kind=kOutput, calls=%fused_computation.90.clone.1 | convolution fusion | flops 408348672 | bytes 7964160 | tf_op jit(solution)/shard_map/transpose(jvp())/while/body/eval_jaxpr/hts,shp->thp/dot_general | solution.py:37
  181.8 3.2 reduce-window.62
  194.8 3.7 fusion.140
  209.4 6.5 %fusion.136 = (f32[8,256]{1,0:T(8,128)}, f32[8,256]{1,0:T(8,128)}, f32[256,256]{1,0:T(8,128)S(1)}, f32[8,256]{1,0:T(8,128)}) fusion(f32[4,8,256,256]{3,2,1,0:T(8,128)} %get-tuple-element.2652, s32[]{:T(128)S(6)} %sub.159, f32[256,256]{1,0:T(8,128)S(1)} %bitcast.499, f32[8,256]{1,0:T(8,128)S(1)} %dynamic-slice_bitcast_fusion.9, ...), kind=kOutput, calls=%fused_computation.90.clone.1 | convolution fusion | flops 408348672 | bytes 7964160 | tf_op jit(solution)/shard_map/transpose(jvp())/while/body/eval_jaxpr/hts,shp->thp/dot_general | solution.py:37
  234.1 3.7 fusion.140
  248.7 6.5 %fusion.136 = (f32[8,256]{1,0:T(8,128)}, f32[8,256]{1,0:T(8,128)}, f32[256,256]{1,0:T(8,128)S(1)}, f32[8,256]{1,0:T(8,128)}) fusion(f32[4,8,256,256]{3,2,1,0:T(8,128)} %get-tuple-element.2652, s32[]{:T(128)S(6)} %sub.159, f32[256,256]{1,0:T(8,128)S(1)} %bitcast.499, f32[8,256]{1,0:T(8,128)S(1)} %dynamic-slice_bitcast_fusion.9, ...), kind=kOutput, calls=%fused_computation.90.clone.1 | convolution fusion | flops 408348672 | bytes 7964160 | tf_op jit(solution)/shard_map/transpose(jvp())/while/body/eval_jaxpr/hts,shp->thp/dot_general | solution.py:37
  273.4 3.7 fusion.140
  288.0 6.5 %fusion.136 = (f32[8,256]{1,0:T(8,128)}, f32[8,256]{1,0:T(8,128)}, f32[256,256]{1,0:T(8,128)S(1)}, f32[8,256]{1,0:T(8,128)}) fusion(f32[4,8,256,256]{3,2,1,0:T(8,128)} %get-tuple-element.2652, s32[]{:T(128)S(6)} %sub.159, f32[256,256]{1,0:T(8,128)S(1)} %bitcast.499, f32[8,256]{1,0:T(8,128)S(1)} %dynamic-slice_bitcast_fusion.9, ...), kind=kOutput, calls=%fused_computation.90.clone.1 | convolution fusion | flops 408348672 | bytes 7964160 | tf_op jit(solution)/shard_map/transpose(jvp())/while/body/eval_jaxpr/hts,shp->thp/dot_general | solution.py:37
  312.7 3.7 fusion.140
  329.8 39.8 %all-reduce.2 = (f32[32]{0:T(128)}, f32[32]{0:T(128)}, f32[32]{0:T(128)}) all-reduce(f32[32]{0:T(128)S(1)} %reshape.486, f32[32]{0:T(128)S(1)} %reshape.487, f32[32]{0:T(128)S(1)} %reshape.488), channel_id=1, replica_groups=mesh['gx'=4,'gy'=2,'gz'=4] {'gx','gy','gz'}, use_global_device_ids=true, to_apply=%region_22.23 | all-reduce | flops 96 | bytes 768 | tf_op jit(solution)/shard_map/psum | solution.py:155
  (332 shorter events, 200.8 us)
Async XLA Ops:
  7.2 11.3 %copy-start = (bf16[256,128]{1,0:T(8,128)(2,1)S(1)}, bf16[256,128]{1,0:T(8,128)(2,1)}, u32[]{:S(2)}) copy-start(bf16[256,128]{1,0:T(8,128)(2,1)} %param.18) | copy-start | bytes 196612
  10.4 11.8 %all-to-all-start.1 = ((f32[1,32,4]{1,0,2:T(1,128)}), f32[1,32,4]{1,0,2:T(1,128)S(1)}, u32[]{:S(2)}, u32[]{:S(2)}) async-start(f32[1,32,4]{1,0,2:T(1,128)} %broadcast_in_dim.201), calls=%async_computation.1 | async-start | bytes 4096 | tf_op jit(solution)/shard_map/all_to_all | solution.py:111
  22.2 29.2 %all-to-all-start = ((f32[1,32,64,128]{3,1,0,2:T(8,128)}), f32[1,32,64,128]{3,1,0,2:T(8,128)S(1)}, u32[]{:S(2)}, u32[]{:S(2)}) async-start(f32[1,32,64,128]{3,1,0,2:T(8,128)} %copy.131), calls=%async_computation | async-start | bytes 2097152 | tf_op jit(solution)/shard_map/all_to_all | solution.py:112
  26.3 53.8 %all-gather.3.cloned.1.call-start = ((), (), s32[]{:S(2)}) async-start(), calls=%async_computation.4 | async-start | bytes 2359296 | tf_op jit(solution)/shard_map/all_gather | solution.py:11
  26.8 26.2 %copy-start.13 = (f32[32]{0:T(128)}, f32[32]{0:T(128)S(1)}, u32[]{:S(2)}) copy-start(f32[32]{0:T(128)S(1)} %get-tuple-element.2004) | copy-start | bytes 388
  27.3 29.4 %copy-start.15 = (f32[32]{0:T(128)S(1)}, f32[32]{0:T(128)}, u32[]{:S(2)}) copy-start(f32[32]{0:T(128)} %param.20) | copy-start | bytes 388
  27.3 29.5 %copy-start.19 = (f32[32]{0:T(128)S(1)}, f32[32]{0:T(128)}, u32[]{:S(2)}) copy-start(f32[32]{0:T(128)} %param.19) | copy-start | bytes 388
  53.0 6.5 %copy-start.20 = (f32[32]{0:T(128)S(1)}, f32[32]{0:T(128)}, u32[]{:S(2)}) copy-start(f32[32]{0:T(128)} %param.21) | copy-start | bytes 388
  53.0 6.6 %copy-start.8 = (bf16[256,128]{1,0:T(8,128)(2,1)S(1)}, bf16[256,128]{1,0:T(8,128)(2,1)}, u32[]{:S(2)}) copy-start(bf16[256,128]{1,0:T(8,128)(2,1)} %param.17) | copy-start | bytes 196612
  53.0 37.5 %all-to-all-start.3 = ((bf16[4,32,16,128]{3,2,1,0:T(8,128)(2,1)}), bf16[4,32,16,128]{3,2,1,0:T(8,128)(2,1)S(1)}, u32[]{:S(2)}, u32[]{:S(2)}) async-start(bf16[4,32,16,128]{3,2,1,0:T(8,128)(2,1)} %param.22), calls=%async_computation.3 | async-start | bytes 1048576 | tf_op jit(solution)/shard_map/all_to_all | solution.py:93
  80.0 9.1 %copy-start.14 = (f32[32]{0:T(128)S(1)}, f32[32]{0:T(128)}, u32[]{:S(2)}) copy-start(f32[32]{0:T(128)} %copy-done.13) | copy-start | bytes 388
  80.0 9.1 %copy-start.16 = (f32[32]{0:T(128)S(1)}, f32[32]{0:T(128)}, u32[]{:S(2)}) copy-start(f32[32]{0:T(128)} %get-tuple-element.2005) | copy-start | bytes 388
  80.0 9.1 %copy-start.17 = (f32[32]{0:T(128)S(1)}, f32[32]{0:T(128)}, u32[]{:S(2)}) copy-start(f32[32]{0:T(128)} %get-tuple-element.1985) | copy-start | bytes 388
  80.0 9.1 %copy-start.18 = (f32[32]{0:T(128)S(1)}, f32[32]{0:T(128)}, u32[]{:S(2)}) copy-start(f32[32]{0:T(128)} %get-tuple-element.1986) | copy-start | bytes 388
  90.5 9.9 %copy-start.7 = (f32[256,32]{0,1:T(8,128)S(1)}, f32[256,32]{0,1:T(8,128)}, u32[]{:S(2)}) copy-start(f32[256,32]{0,1:T(8,128)} %param.16) | copy-start | bytes 98308
  90.5 6.3 %copy-start.5 = (bf16[4,32,16,128]{3,2,1,0:T(8,128)(2,1)}, bf16[4,32,16,128]{3,2,1,0:T(8,128)(2,1)S(1)}, u32[]{:S(2)}) copy-start(bf16[4,32,16,128]{3,2,1,0:T(8,128)(2,1)S(1)} %all-to-all-done.3) | copy-start | bytes 1572868
  90.5 68.1 %all-to-all-start.2 = ((f32[4,32,16,128]{3,2,1,0:T(8,128)}), f32[4,32,16,128]{3,2,1,0:T(8,128)}, u32[]{:S(2)}, u32[]{:S(2)}) async-start(f32[4,32,16,128]{3,2,1,0:T(8,128)} %pad_maximum_fusion), calls=%async_computation.2 | async-start | bytes 2097152 | tf_op jit(solution)/shard_map/all_to_all | solution.py:134
  194.8 3.8 %copy-start.12 = (f32[8]{0:T(128)S(1)}, f32[8]{0:T(128)}, u32[]{:S(2)}) copy-start(f32[8]{0:T(128)} %get-tuple-element.2442) | copy-start | bytes 100 | tf_op jit(solution)/shard_map/transpose(jvp())/while
  198.5 5.6 %copy-start.11 = (f32[4,8]{0,1:T(8,128)S(1)}, f32[4,8]{0,1:T(8,128)}, u32[]{:S(2)}) copy-start(f32[4,8]{0,1:T(8,128)} %copy-done.10) | copy-start | bytes 388 | tf_op jit(solution)/shard_map/transpose(jvp())/while
  237.8 5.7 %copy-start.11 = (f32[4,8]{0,1:T(8,128)S(1)}, f32[4,8]{0,1:T(8,128)}, u32[]{:S(2)}) copy-start(f32[4,8]{0,1:T(8,128)} %copy-done.10) | copy-start | bytes 388 | tf_op jit(solution)/shard_map/transpose(jvp())/while
  277.1 5.7 %copy-start.11 = (f32[4,8]{0,1:T(8,128)S(1)}, f32[4,8]{0,1:T(8,128)}, u32[]{:S(2)}) copy-start(f32[4,8]{0,1:T(8,128)} %copy-done.10) | copy-start | bytes 388 | tf_op jit(solution)/shard_map/transpose(jvp())/while
  316.4 5.7 %copy-start.11 = (f32[4,8]{0,1:T(8,128)S(1)}, f32[4,8]{0,1:T(8,128)}, u32[]{:S(2)}) copy-start(f32[4,8]{0,1:T(8,128)} %copy-done.10) | copy-start | bytes 388 | tf_op jit(solution)/shard_map/transpose(jvp())/while
  322.1 47.5 %copy-start.2 = (f32[4,256,8,64]{1,3,2,0:T(8,128)S(1)}, f32[4,256,8,64]{1,3,2,0:T(8,128)}, u32[]{:S(2)}) copy-start(f32[4,256,8,64]{1,3,2,0:T(8,128)} %get-tuple-element.1166) | copy-start | bytes 6291460
  322.1 47.5 %copy-start.4 = (bf16[4,32,16,128]{3,2,0,1:T(8,128)(2,1)S(1)}, bf16[4,32,16,128]{3,2,0,1:T(8,128)(2,1)}, u32[]{:S(2)}) copy-start(bf16[4,32,16,128]{3,2,0,1:T(8,128)(2,1)} %copy-done.3) | copy-start | bytes 1572868
  (11 other events, 20.9 us)
Sparse Core Ops, SparseCore 0:
  53.1 26.8 all-gather.2
where the time goes:
time: 383 us; the launch traced here: 379 us
  other arithmetic  98.9 us (26%)
  local copies, waits for them, and re-layouts  90.7 us (24%)
  matrix products  70.4 us (18%)
  blocking collectives  52.1 us (14%)
  waiting for transfers between devices  33.1 us (9%)
  starting transfers between devices  18.7 us (5%)
  between operations  14.4 us (4%)
    dot_general x8, matrix products, block_forward(): inner = jnp.einsum('hts,shp->thp', mix, inputs, precision=highest)  40.7 us
    psum x1, blocking collectives, local(): lax.psum((grads[5], grads[6], grads[7]), ('gx', 'gy', 'gz'))  39.8 us
    dynamic_update_slice x24, other arithmetic, span_forward(): lax.map(one_block, (grouped, raw_g, read_g, decay_log.reshape(blocks, blo...  30.3 us
    dynamic_update_slice x36, local copies, waits for them, and re-layouts, span_forward(): lax.map(one_block, (grouped, raw_g, read_g, decay_log.reshape(blocks, blo...  30 us
    another operation x33, other arithmetic  27.8 us
    all_to_all x1, waiting for transfers between devices, local(): lax.all_to_all(local_term[None], 'gz', split_axis=2, concat_axis=0, tiled...  24.1 us
    dot_general x8, matrix products, block_forward(): jnp.einsum('sh,shp,sn->hpn', tail, inputs, b_mat, precision=highest)  21.1 us
    another operation x30, local copies, waits for them, and re-layouts  15.2 us
  transfers between devices with their start and end apart: 5, of which 3 were waited for; matrix products, arithmetic and copies ran while one was open for 22% of the time, Pallas kernels for 0%

commit v1 on v0

v1 whole, which is shorter than its diff:
```python
import functools
import math

import jax
import jax.numpy as jnp
from jax import lax
from jax.experimental import pallas as pl
from jax.experimental.pallas import tpu as pltpu
from jax.sharding import PartitionSpec as P

F32, BF16 = jnp.float32, jnp.bfloat16
AXES = ("gx", "gy", "gz")
LOG2E = math.log2(math.e)
LANES = 128
NT = (((1,), (1,)), ((), ()))
TN = (((0,), (0,)), ((), ()))


def dot(a, b, dims=(((1,), (0,)), ((), ()))):
    return lax.dot_general(a, b, dims, preferred_element_type=F32)


def halves(a):
    hi = a.astype(BF16)
    return hi, (a - hi.astype(F32)).astype(BF16)


def thirds(a):
    hi = a.astype(BF16)
    rest = a - hi.astype(F32)
    mid = rest.astype(BF16)
    return hi, mid, (rest - mid.astype(F32)).astype(BF16)


def column(a, h):
    return pltpu.roll(a, lax.rem(LANES - h, LANES), 1)[:, 0:1]


def low_lanes(shape, width):
    return lax.broadcasted_iota(jnp.int32, shape, 1) < width


def pair_columns(a, j, width):
    first, second = column(a, 2 * j), column(a, 2 * j + 1)
    return jnp.where(low_lanes((a.shape[0], 2 * width), width), first, second)


def head_sum(prod, j, width):
    hi, lo = halves(prod)
    rows = lax.broadcasted_iota(jnp.int32, (4 * width, LANES), 0)
    lanes = lax.broadcasted_iota(jnp.int32, (4 * width, LANES), 1)
    head = 2 * j + jnp.where(lax.rem(rows, 2 * width) >= width, 1, 0)
    pick = jnp.where(lanes == head, 1.0, 0.0).astype(BF16)
    return dot(jnp.concatenate([hi, lo], 1), pick)


def first_kernel(
    rows, raw_ref, par_ref, g_ref, c_ref, cum_ref, dt_ref, cumt_ref, block_ref, ecum, ecumt
):
    length, heads = raw_ref.shape
    wide = g_ref.shape[1]
    width = wide // heads
    par = par_ref[...]
    z = raw_ref[...] + par[1:2, :heads]
    dt = jnp.maximum(z, 0.0) + jnp.log1p(jnp.exp(-jnp.abs(z)))
    dt_ref[...] = jnp.zeros(dt_ref.shape, F32)
    dt_ref[:, :heads] = dt
    dt = dt_ref[...]
    a = dt * -jnp.exp(par[0:1, :])
    r = lax.broadcasted_iota(jnp.int32, (length, length), 0)
    c = lax.broadcasted_iota(jnp.int32, (length, length), 1)
    lower = jnp.where(r >= c, 1.0, 0.0).astype(BF16)
    hi, mid, lo = thirds(a)
    cum = dot(lower, hi) + (dot(lower, mid) + dot(lower, lo))
    cum = cum * LOG2E
    cum_ref[...] = cum
    cumt = cum.T
    cumt_ref[...] = cumt
    ecum[...] = jnp.exp2(cum)
    ecumt[...] = jnp.exp2(cumt)
    cc = c_ref[...]
    c2 = jnp.concatenate([cc, cc], 0)
    per = 2 * width // rows

    def body(j, _):
        at = pl.ds(pl.multiple_of(j * 2 * width, 2 * width), 2 * width)
        weighted = g_ref[:, at].astype(F32) * pair_columns(ecum[...], j, width)
        hi, lo = halves(weighted)
        state = dot(jnp.concatenate([hi, lo], 0), c2, TN)
        for i in range(per):
            head = 2 * j + (i * rows) // width
            block_ref[j * per + i, 0:rows, :] = state[i * rows : (i + 1) * rows]
            decay = ecumt[pl.ds(head, 1), :][:, length - 1 : length]
            block_ref[j * per + i, rows : rows + 8, :] = jnp.broadcast_to(decay, (8, LANES))
        return 0

    lax.fori_loop(0, heads // 2, body, 0)


def scan_kernel(rows, got_ref, carry_ref):
    n = got_ref.shape[0]

    def hop(k, acc):
        at = n - 1 - k
        carry_ref[at] = acc
        part = got_ref[at]
        return part[0:rows] + part[rows : rows + 1] * acc

    lax.fori_loop(0, n, hop, jnp.zeros((rows, LANES), F32))


def inner_kernel(
    x_ref, g_ref, b_ref, c_ref, cum_ref, dt_ref, cumt_ref,
    dxi_ref, cole_ref, bg_ref, cg_ref, skip_ref, gt, dg
):
    length, wide = x_ref.shape
    heads = 2 * wide // LANES
    width = wide // heads
    half = length // 2
    r = lax.broadcasted_iota(jnp.int32, (length, length), 0)
    c = lax.broadcasted_iota(jnp.int32, (length, length), 1)
    gt[...] = jnp.where(c >= r, dot(b_ref[...], c_ref[...], NT), 0.0)
    dg[...] = jnp.zeros(dg.shape, F32)
    cole_ref[...] = jnp.zeros(cole_ref.shape, F32)
    skip_ref[...] = jnp.zeros(skip_ref.shape, F32)
    lanes = lax.broadcasted_iota(jnp.int32, (1, 2 * width), 1)
    masks_f = [jnp.where(lanes < width, 1.0, 0.0), jnp.where(lanes < width, 0.0, 1.0)]
    masks = [m.astype(BF16) for m in masks_f]

    def body(j, _):
        at = pl.ds(pl.multiple_of(j * 2 * width, 2 * width), 2 * width)
        xp, gp = x_ref[:, at], g_ref[:, at]
        gs = [gp * m for m in masks]
        overlap = jnp.sum(xp.astype(F32) * gp.astype(F32), 0, keepdims=True)
        sums = []
        parts = [[], []]
        for k in range(2):
            h = 2 * j + k
            cs, ds = column(cum_ref[...], h), column(dt_ref[...], h)
            ct = cumt_ref[pl.ds(h, 1), :]
            xk = xp * masks[k]
            skip_ref[pl.ds(h, 1), :] = overlap * masks_f[k]
            total = None
            for q in range(2):
                s0 = q * half
                rs, ts = slice(s0, s0 + half), slice(s0, length)
                dm = dot(xk[rs], gp[ts], NT)
                low = jnp.exp2(jnp.minimum(ct[:, ts] - cs[rs], 0.0))
                scores = gt[rs, ts]
                parts[q] += list(halves(low * scores))
                dl = dm * (low * ds[rs])
                dg[rs, ts] += dl
                part = jnp.sum(dl * scores, 0, keepdims=True)
                if q == 0:
                    total = part
                else:
                    total = jnp.concatenate([total[:, :half], total[:, half:] + part], 1)
            cole_ref[pl.ds(h, 1), :] = total
        for q in range(2):
            s0 = q * half
            rhs = jnp.concatenate([gs[0][s0:], gs[0][s0:], gs[1][s0:], gs[1][s0:]], 0)
            dxi_ref[s0 : s0 + half, at] = dot(jnp.concatenate(parts[q], 1), rhs)
        return 0

    lax.fori_loop(0, heads // 2, body, 0)
    d = jnp.where(c >= r, dg[...], 0.0)
    bb, cc = b_ref[...], c_ref[...]
    bg_ref[...] = dot(jnp.concatenate(halves(d), 1), jnp.concatenate([cc, cc], 0))
    cg_ref[...] = dot(jnp.concatenate(halves(d.T), 1), jnp.concatenate([bb, bb], 0))


def read_kernel(g_ref, c_ref, start_ref, cum_ref, cg_in, cg_ref, gr_ref, ecum, hi_ref, lo_ref):
    length, wide = g_ref.shape
    heads, width = start_ref.shape[0], start_ref.shape[1]
    ecum[...] = jnp.exp2(cum_ref[...])
    gr_ref[...] = jnp.zeros(gr_ref.shape, F32)
    cc = c_ref[...]

    def body(j, cg):
        at = pl.ds(pl.multiple_of(j * 2 * width, 2 * width), 2 * width)
        gp = g_ref[:, at].astype(F32)
        hp = start_ref[pl.ds(2 * j, 2)].reshape(2 * width, LANES)
        gr_ref[...] += head_sum(gp * dot(cc, hp, NT), j, width)
        hi, lo = halves(gp * pair_columns(ecum[...], j, width))
        return cg + dot(jnp.concatenate([hi, lo], 1), jnp.concatenate([hp, hp], 0))

    cg_ref[...] = lax.fori_loop(0, heads // 2, body, cg_in[...])


def last_kernel(
    x_ref, g_ref, b_ref, raw_ref, par_ref, start_ref, later_ref, cum_ref, dt_ref,
    dxi_ref, cole_ref, gr_ref, skip_ref, bg_in,
    dx_ref, draw_ref, bg_ref, part_ref, tail, ddt, ends
):
    length, wide = x_ref.shape
    heads, width = start_ref.shape[0], start_ref.shape[1]
    cum = cum_ref[...]
    tail[...] = jnp.exp2(cum[length - 1 : length] - cum)
    ddt[...] = jnp.zeros(ddt.shape, F32)
    ends[...] = jnp.zeros(ends.shape, F32)
    bb = b_ref[...]
    b2 = jnp.concatenate([bb, bb], 1)
    lanes = lax.broadcasted_iota(jnp.int32, (1, 2 * width), 1)
    masks_f = [jnp.where(lanes < width, 1.0, 0.0), jnp.where(lanes < width, 0.0, 1.0)]
    par = par_ref[...]

    def body(j, bg):
        at = pl.ds(pl.multiple_of(j * 2 * width, 2 * width), 2 * width)
        xp, gp = x_ref[:, at].astype(F32), g_ref[:, at].astype(F32)
        later = later_ref[pl.ds(2 * j, 2)].reshape(2 * width, LANES)
        hp = start_ref[pl.ds(2 * j, 2)].reshape(2 * width, LANES).astype(F32)
        lhi, llo = halves(later)
        u = dot(b2, jnp.concatenate([lhi, llo], 1), NT)
        tp, dtp = pair_columns(tail[...], j, width), pair_columns(dt_ref[...], j, width)
        skips = pair_columns(par, j, width)[2:3]
        tu = tp * u
        v = dxi_ref[:, at] + tu
        ddt[...] += head_sum(xp * v, j, width)
        dx_ref[:, at] = (dtp * v + skips * gp).astype(BF16)
        dx_w = dtp * xp
        cross = later * hp
        out = jnp.sum(dx_w * tu, 0, keepdims=True)
        for k in range(2):
            h = 2 * j + k
            own = jnp.sum(cross[k * width : (k + 1) * width], 0, keepdims=True)
            decay = jnp.exp2(column(cum_ref[length - 8 : length, :], h))[7:8]
            ends[pl.ds(h, 1), :] = own * decay + out * masks_f[k]
        whi, wlo = halves(tp * dx_w)
        return bg + dot(
            jnp.concatenate([whi, wlo, whi], 1), jnp.concatenate([lhi, lhi, llo], 0)
        )

    bg_ref[...] = lax.fori_loop(0, heads // 2, body, bg_in[...])
    dt = dt_ref[...]
    dd = ddt[...]
    dcum = cole_ref[...].T + jnp.exp2(cum) * gr_ref[...] - dt * dd
    r = lax.broadcasted_iota(jnp.int32, (length, length), 0)
    c = lax.broadcasted_iota(jnp.int32, (length, length), 1)
    upper = jnp.where(c >= r, 1.0, 0.0).astype(BF16)
    hi, mid, lo = thirds(dcum)
    da = dot(upper, hi) + (dot(upper, mid) + dot(upper, lo))
    da = da + jnp.sum(ends[...].T, 0, keepdims=True)
    rate = -jnp.exp(par[0:1])
    total = (dd + da * rate)[:, :heads]
    draw = total * jax.nn.sigmoid(raw_ref[...] + par[1:2, :heads])
    draw_ref[...] = draw
    part_ref[...] = jnp.zeros(part_ref.shape, F32)
    part_ref[0:1, :] = jnp.sum(da * dt, 0, keepdims=True) * rate
    part_ref[1:2, :heads] = jnp.sum(draw, 0, keepdims=True)
    part_ref[2:3, :] = jnp.sum(skip_ref[...].T, 0, keepdims=True)


def call(body, outs, scratch=(), flops=0, moved=0):
    return pl.pallas_call(
        body,
        out_shape=[jax.ShapeDtypeStruct(s, d) for s, d in outs],
        scratch_shapes=[pltpu.VMEM(s, F32) for s in scratch],
        compiler_params=pltpu.CompilerParams(vmem_limit_bytes=48 * 1024 * 1024),
        cost_estimate=pl.CostEstimate(flops=flops, bytes_accessed=moved, transcendentals=0),
    )


def local(n, x, raw, b_mat, c_mat, decay_log, bias, skip, checkpoints, grad):
    length, heads = raw.shape
    wide = x.shape[1]
    width = wide // heads
    states = b_mat.shape[1]
    rows = wide // n
    assert states == LANES and 2 * width == LANES and width % rows == 0
    entering = lax.all_to_all(checkpoints, "gz", split_axis=0, concat_axis=2, tiled=True)[0]
    par = jnp.pad(jnp.stack([decay_log, bias, skip]), ((0, 5), (0, LANES - heads)))
    tok = (length, LANES)
    tok_t = (LANES, length)
    cum, dt, cumt, blocks = call(
        functools.partial(first_kernel, rows),
        [(tok, F32), (tok, F32), (tok_t, F32), ((n, rows + 8, LANES), F32)],
        [tok, tok_t],
        flops=4 * length * wide * LANES,
    )(raw, par, grad, c_mat)
    got = lax.all_to_all(blocks, AXES, split_axis=0, concat_axis=0, tiled=True)
    dxi, cole, bg, cg, skips = call(
        inner_kernel,
        [((length, wide), F32), (tok_t, F32), (tok, F32), (tok, F32), ((LANES, LANES), F32)],
        [(length, length), (length, length)],
        flops=40 * length * wide * LANES,
    )(x, grad, b_mat, c_mat, cum, dt, cumt)
    (carry,) = call(
        functools.partial(scan_kernel, rows), [((n, rows, LANES), F32)]
    )(got)
    later = lax.all_to_all(carry, AXES, split_axis=0, concat_axis=0, tiled=True)
    later = later.reshape(heads, width, states)
    cg, gr = call(
        read_kernel,
        [(tok, F32), (tok, F32)],
        [tok, tok, tok],
        flops=16 * length * wide * LANES,
    )(grad, c_mat, entering, cum, cg)
    dx, draw, bg, part = call(
        last_kernel,
        [((length, wide), BF16), ((length, heads), F32), (tok, F32), ((8, LANES), F32)],
        [tok, tok, (LANES, LANES)],
        flops=16 * length * wide * LANES,
    )(x, grad, b_mat, raw, par, entering, later, cum, dt, dxi, cole, gr, skips, bg)
    total = lax.psum(part, AXES)
    return dx, draw, bg, cg, total[0, :heads], total[1, :heads], total[2, :heads]


def solution(mesh):
    tokens = P(AXES, None)
    n = math.prod(mesh.shape[a] for a in AXES)
    return jax.shard_map(
        functools.partial(local, n),
        mesh=mesh,
        in_specs=(tokens,) * 4 + (P(),) * 3 + (P(("gx", "gy"), None, "gz", None), tokens),
        out_specs=(tokens,) * 4 + (P(),) * 3,
        check_vma=False,
    )
```

time: 383 us -> 153 us (0.40)
  other arithmetic: 98.9 us -> 0.7 us
  local copies, waits for them, and re-layouts: 90.7 us -> 11 us
  matrix products: 70.4 us -> 0 us
  Pallas kernels: 0 us -> 35.8 us
  blocking collectives: 52.1 us -> 76.7 us
  between operations: 14.4 us -> 0.73 us
  starting transfers between devices: 18.7 us -> 6.12 us
  waiting for transfers between devices: 33.1 us -> 21 us
    dot_general x22 -> x0, matrix products: 70.4 us -> none  [the longest x8 40.7 us: block_forward(): inner = jnp.einsum('hts,shp->thp', mix, inputs, precision=highest)]
    all_to_all x0 -> x1, blocking collectives: none -> 37.8 us  [local(): got = lax.all_to_all(blocks, AXES, split_axis=0, concat_axis=0, tiled=True)]
    pallas_call x0 -> x5, Pallas kernels: none -> 35.8 us  [the longest x1 11 us: local(): call(last_kernel, [((length, wide), BF16), ((length, heads), F32), (tok,...]
    dynamic_update_slice x24 -> x0, other arithmetic: 30.3 us -> none  [span_forward(): lax.map(one_block, (grouped, raw_g, read_g, decay_log.reshape(blocks, blo...]
    dynamic_update_slice x36 -> x0, local copies, waits for them, and re-layouts: 30 us -> none  [span_forward(): lax.map(one_block, (grouped, raw_g, read_g, decay_log.reshape(blocks, blo...]
    another operation x35 -> x1, other arithmetic: 29.1 us -> 0.7 us  [local(): jnp.stack([decay_log, bias, skip])]
    all_to_all x3 -> x1, waiting for transfers between devices: 25.2 us -> 7.13 us  [local(): later = lax.all_to_all(carry, AXES, split_axis=0, concat_axis=0, tiled=True)]
    reduce_sum x12 -> x0, other arithmetic: 15.8 us -> none  [the longest x4 6.75 us: block_forward(): jnp.exp(cum[-1])[:, None, None] * start]
  transfers between devices with their start and end apart: 5 -> 2, of which waited for: 3 -> 2; matrix products, arithmetic and copies ran while one was open for 22% -> 0% of each run, Pallas kernels for 0% -> 12%
where the time goes in v1:
time: 153 us; the launch traced here: 152 us
  blocking collectives  76.7 us (50%)
  Pallas kernels  35.8 us (23%)
  waiting for transfers between devices  21 us (14%)
  local copies, waits for them, and re-layouts  11 us (7%)
  starting transfers between devices  6.12 us (4%)
    psum x1, blocking collectives, local(): total = lax.psum(part, AXES)  38.9 us
    all_to_all x1, blocking collectives, local(): got = lax.all_to_all(blocks, AXES, split_axis=0, concat_axis=0, tiled=True)  37.8 us
    all_to_all x1, waiting for transfers between devices, local(): lax.all_to_all(checkpoints, 'gz', split_axis=0, concat_axis=2, tiled=True)  13.8 us
    pallas_call x1, Pallas kernels, local(): call(last_kernel, [((length, wide), BF16), ((length, heads), F32), (tok,...  11 us
    unnamed x28, local copies, waits for them, and re-layouts  10.4 us
    pallas_call x1, Pallas kernels, local(): call(inner_kernel, [((length, wide), F32), (tok_t, F32), (tok, F32), (tok...  9.61 us
    pallas_call x1, Pallas kernels, local(): call(functools.partial(first_kernel, rows), [(tok, F32), (tok, F32), (tok...  7.22 us
    all_to_all x1, waiting for transfers between devices, local(): later = lax.all_to_all(carry, AXES, split_axis=0, concat_axis=0, tiled=True)  7.13 us
  transfers between devices with their start and end apart: 2, of which 2 were waited for; matrix products, arithmetic and copies ran while one was open for 0% of the time, Pallas kernels for 12%

profile of v1, /device:TPU:0, one launch (start us, length us, event | category | flops | bytes accessed | tf_op | source)
XLA Modules:
  0.0 152.0 jit_solution(13636541563314954267)
XLA Ops:
  0.6 0.9 copy.18.raw_ref
  1.5 0.7 select_maximum_fusion.par_ref
  2.2 1.2 copy-done
  3.4 0.8 copy-done.9
  4.3 7.2 %shard_map.144 = (f32[256,128]{1,0:T(8,128)S(1)}, f32[256,128]{1,0:T(8,128)S(1)}, f32[128,256]{1,0:T(8,128)S(1)}, f32[32,72,128]{2,1,0:T(8,128)S(1)}) custom-call(f32[256,32]{1,0:T(8,128)S(1)} %copy.18.raw_ref, f32[8,128]{1,0:T(8,128)S(1)} %select_maximum_fusion.par_ref, bf16[256,2048]{1,0:T(8,128)(2,1)S(1)} %copy-done, bf16[256,128]{1,0:T(8,128)(2,1)S(1)} %copy-done.9), custom_call_target="tpu_custom_call" | custom-call | flops 268435456 | tf_op jit(solution)/shard_map/pallas_call | solution.py:274
  11.5 37.8 %all_to_all.25.got_ref = f32[32,72,128]{2,1,0:T(8,128)S(1)} all-to-all(f32[32,72,128]{2,1,0:T(8,128)S(1)} %get-tuple-element.22), channel_id=1, replica_groups=mesh['gx'=4,'gy'=2,'gz'=4] {'gx','gy','gz'}, dimensions={0} | all-to-all | bytes 2359296 | tf_op jit(solution)/shard_map/all_to_all | solution.py:280
  49.2 3.5 %all-to-all-start = ((bf16[4,32,16,128]{3,2,1,0:T(8,128)(2,1)}), bf16[4,32,16,128]{3,2,1,0:T(8,128)(2,1)S(1)}, u32[]{:S(2)}, u32[]{:S(2)}) async-start(bf16[4,32,16,128]{3,2,1,0:T(8,128)(2,1)} %param.16), calls=%async_computation | async-start | bytes 1048576 | tf_op jit(solution)/shard_map/all_to_all | solution.py:270
  52.7 1.2 shard_map.145
  53.9 13.8 %all-to-all-done = bf16[4,32,16,128]{3,2,1,0:T(8,128)(2,1)S(1)} async-done(((bf16[4,32,16,128]{3,2,1,0:T(8,128)(2,1)}), bf16[4,32,16,128]{3,2,1,0:T(8,128)(2,1)S(1)}, u32[]{:S(2)}, u32[]{:S(2)}) %all-to-all-start) | async-done | bytes 524320 | tf_op jit(solution)/shard_map/all_to_all | solution.py:270
  67.7 0.8 copy-done.11
  68.5 2.6 %all-to-all-start.2 = ((f32[32,64,128]{2,1,0:T(8,128)}), f32[32,64,128]{2,1,0:T(8,128)S(1)}, u32[]{:S(2)}, u32[]{:S(2)}) async-start(f32[32,64,128]{2,1,0:T(8,128)} %shard_map.145), calls=%async_computation.2 | async-start | bytes 2097152 | tf_op jit(solution)/shard_map/all_to_all | solution.py:290
  71.2 1.2 copy-done.3
  72.5 9.6 %shard_map.146 = (f32[256,2048]{1,0:T(8,128)S(1)}, f32[128,256]{1,0:T(8,128)S(1)}, f32[256,128]{1,0:T(8,128)S(1)}, f32[256,128]{1,0:T(8,128)S(1)}, f32[128,128]{1,0:T(8,128)S(1)}) custom-call(bf16[256,2048]{1,0:T(8,128)(2,1)S(1)} %copy-done.3, bf16[256,2048]{1,0:T(8,128)(2,1)S(1)} %copy-done.1, bf16[256,128]{1,0:T(8,128)(2,1)S(1)} %copy-done.5, ...), custom_call_target="tpu_custom_call" | custom-call | flops 2684354560 | tf_op jit(solution)/shard_map/pallas_call | solution.py:281
  82.1 1.3 copy-done.2
  83.5 0.6 copy-done.7
  84.1 6.8 %shard_map.147 = (f32[256,128]{1,0:T(8,128)}, f32[256,128]{1,0:T(8,128)S(1)}) custom-call(bf16[256,2048]{1,0:T(8,128)(2,1)S(1)} %copy-done.1, bf16[256,128]{1,0:T(8,128)(2,1)S(1)} %copy-done.10, bf16[32,64,128]{2,1,0:T(8,128)(2,1)S(1)} %bitcast.13, f32[256,128]{1,0:T(8,128)S(1)} %get-tuple-element.23.cum_ref, f32[256,128]{1,0:T(8,128)S(1)} %get-tuple-element.28.cg_in), custom_call_target="tpu_custom_call" | custom-call | flops 1073741824 | tf_op jit(solution)/shard_map/pallas_call | solution.py:292
  90.8 7.1 %all-to-all-done.2.later_ref = f32[32,64,128]{2,1,0:T(8,128)S(1)} async-done(((f32[32,64,128]{2,1,0:T(8,128)}), f32[32,64,128]{2,1,0:T(8,128)S(1)}, u32[]{:S(2)}, u32[]{:S(2)}) %all-to-all-start.2) | async-done | bytes 1048608 | tf_op jit(solution)/shard_map/all_to_all | solution.py:290
  98.0 1.2 copy-done.4
  99.2 0.8 copy-done.6
  100.0 0.8 copy-done.8
  100.9 11.0 %shard_map.148 = (bf16[256,2048]{1,0:T(8,128)(2,1)}, f32[256,32]{1,0:T(8,128)S(1)}, f32[256,128]{1,0:T(8,128)}, f32[8,128]{1,0:T(8,128)S(1)}) custom-call(bf16[256,2048]{1,0:T(8,128)(2,1)S(1)} %copy-done.4, bf16[256,2048]{1,0:T(8,128)(2,1)S(1)} %copy-done.1, bf16[256,128]{1,0:T(8,128)(2,1)S(1)} %copy-done.6, f32[256,32]{1,0:T(8,128)S(1)} %copy.18.raw_ref, ...), custom_call_target="tpu_custom_call" | custom-call | flops 1073741824 | tf_op jit(solution)/shard_map/pallas_call | solution.py:298
  111.9 38.9 %psum.7 = f32[8,128]{1,0:T(8,128)S(1)} all-reduce(f32[8,128]{1,0:T(8,128)S(1)} %get-tuple-element.36), channel_id=1, replica_groups=mesh['gx'=4,'gy'=2,'gz'=4] {'gx','gy','gz'}, use_global_device_ids=true, to_apply=%region_0.1 | all-reduce | flops 1024 | bytes 8192 | tf_op jit(solution)/shard_map/psum | solution.py:304
  150.7 0.5 slice_bitcast_fusion
  151.3 0.7 copy.19
  (18 shorter events, 0.1 us)
Async XLA Ops:
  2.2 1.2 copy-start
  3.4 0.8 copy-start.9
  49.2 18.5 %all-to-all-start = ((bf16[4,32,16,128]{3,2,1,0:T(8,128)(2,1)}), bf16[4,32,16,128]{3,2,1,0:T(8,128)(2,1)S(1)}, u32[]{:S(2)}, u32[]{:S(2)}) async-start(bf16[4,32,16,128]{3,2,1,0:T(8,128)(2,1)} %param.16), calls=%async_computation | async-start | bytes 1048576 | tf_op jit(solution)/shard_map/all_to_all | solution.py:270
  53.9 17.3 %copy-start.1 = (bf16[256,2048]{1,0:T(8,128)(2,1)S(1)}, bf16[256,2048]{1,0:T(8,128)(2,1)}, u32[]{:S(2)}) copy-start(bf16[256,2048]{1,0:T(8,128)(2,1)} %g_ref.7) | copy-start | bytes 3145732
  53.9 17.3 %copy-start.5 = (bf16[256,128]{1,0:T(8,128)(2,1)S(1)}, bf16[256,128]{1,0:T(8,128)(2,1)}, u32[]{:S(2)}) copy-start(bf16[256,128]{1,0:T(8,128)(2,1)} %b_ref.3) | copy-start | bytes 196612
  53.9 17.3 %copy-start.10 = (bf16[256,128]{1,0:T(8,128)(2,1)S(1)}, bf16[256,128]{1,0:T(8,128)(2,1)}, u32[]{:S(2)}) copy-start(bf16[256,128]{1,0:T(8,128)(2,1)} %c_ref.5) | copy-start | bytes 196612
  67.7 0.8 copy-start.11
  68.5 29.4 %all-to-all-start.2 = ((f32[32,64,128]{2,1,0:T(8,128)}), f32[32,64,128]{2,1,0:T(8,128)S(1)}, u32[]{:S(2)}, u32[]{:S(2)}) async-start(f32[32,64,128]{2,1,0:T(8,128)} %shard_map.145), calls=%async_computation.2 | async-start | bytes 2097152 | tf_op jit(solution)/shard_map/all_to_all | solution.py:290
  71.2 1.2 copy-start.3
  72.5 11.0 %copy-start.12 = (bf16[4,32,16,128]{3,2,1,0:T(8,128)(2,1)S(1)}, bf16[4,32,16,128]{3,2,1,0:T(8,128)(2,1)}, u32[]{:S(2)}) copy-start(bf16[4,32,16,128]{3,2,1,0:T(8,128)(2,1)} %copy-done.11) | copy-start | bytes 1572868
  82.1 1.3 copy-start.2
  83.4 0.6 copy-start.7
  98.0 1.2 copy-start.4
  99.2 0.8 copy-start.6
  100.0 0.8 copy-start.8

commit v2 on v1

v2 whole, which is shorter than its diff:
```python
import functools
import math

import jax
import jax.numpy as jnp
from jax import lax
from jax.experimental import pallas as pl
from jax.experimental.pallas import tpu as pltpu
from jax.sharding import PartitionSpec as P

F32, BF16 = jnp.float32, jnp.bfloat16
AXES = ("gx", "gy", "gz")
LOG2E = math.log2(math.e)
LANES = 128
NT = (((1,), (1,)), ((), ()))
TN = (((0,), (0,)), ((), ()))


def dot(a, b, dims=(((1,), (0,)), ((), ()))):
    return lax.dot_general(a, b, dims, preferred_element_type=F32)


def halves(a):
    hi = a.astype(BF16)
    return hi, (a - hi.astype(F32)).astype(BF16)


def thirds(a):
    hi = a.astype(BF16)
    rest = a - hi.astype(F32)
    mid = rest.astype(BF16)
    return hi, mid, (rest - mid.astype(F32)).astype(BF16)


def column(a, h):
    return pltpu.roll(a, lax.rem(LANES - h, LANES), 1)[:, 0:1]


def low_lanes(shape, width):
    return lax.broadcasted_iota(jnp.int32, shape, 1) < width


def pair_columns(a, j, width):
    first, second = column(a, 2 * j), column(a, 2 * j + 1)
    return jnp.where(low_lanes((a.shape[0], 2 * width), width), first, second)


def head_sum(prod, j, width):
    hi, lo = halves(prod)
    rows = lax.broadcasted_iota(jnp.int32, (4 * width, LANES), 0)
    lanes = lax.broadcasted_iota(jnp.int32, (4 * width, LANES), 1)
    head = 2 * j + jnp.where(lax.rem(rows, 2 * width) >= width, 1, 0)
    pick = jnp.where(lanes == head, 1.0, 0.0).astype(BF16)
    return dot(jnp.concatenate([hi, lo], 1), pick)


def everything(
    n, sizes, raw_ref, par_ref, b_ref, c_ref, x_hbm, g_hbm, check_hbm,
    dx_hbm, draw_ref, bg_ref, cg_ref, sum_ref,
    x_ref, g_ref, dx_ref, start_ref, block_ref, got_ref, carry_ref, later_ref,
    cum_ref, dt_ref, ecum, tail, gr_ref, ddt, cumt_ref, ecumt, cole_ref, skip_ref, ends,
    gt, dg, dxi_ref, part_ref, parts_ref,
    load_sem, store_sem, check_send, check_recv, block_send, block_recv,
    carry_send, carry_recv, part_send, part_recv,
):
    length, heads = raw_ref.shape
    wide = x_ref.shape[1]
    width = wide // heads
    two = 2 * width
    pairs = heads // 2
    rows = wide // n
    per = two // rows
    half = length // 2
    group = sizes[2]
    zi = lax.axis_index("gz")
    me = (lax.axis_index("gx") * sizes[1] + lax.axis_index("gy")) * group + zi

    def place(d):
        return (
            lax.div(d, sizes[1] * group),
            lax.rem(lax.div(d, group), sizes[1]),
            lax.rem(d, group),
        )

    def remote(src, dst, send, recv, to):
        return pltpu.make_async_remote_copy(
            src_ref=src, dst_ref=dst, send_sem=send, recv_sem=recv,
            device_id=to, device_id_type=pl.DeviceIdType.MESH,
        )

    def other(i):
        return lax.rem(me + i, n)

    load_g = pltpu.make_async_copy(g_hbm, g_ref, load_sem.at[0])
    load_x = pltpu.make_async_copy(x_hbm, x_ref, load_sem.at[1])
    load_g.start()
    load_x.start()
    own_check = pltpu.make_async_copy(check_hbm.at[zi], start_ref.at[zi], load_sem.at[2])
    own_check.start()

    barrier = pltpu.get_barrier_semaphore()

    def greet(i, _):
        pl.semaphore_signal(
            barrier, inc=1, device_id=place(other(i)), device_id_type=pl.DeviceIdType.MESH
        )
        return 0

    lax.fori_loop(1, n, greet, 0)

    par = par_ref[...]
    dt_ref[...] = jnp.zeros(dt_ref.shape, F32)
    z = raw_ref[...] + par[1:2, :heads]
    dt_ref[:, :heads] = jnp.maximum(z, 0.0) + jnp.log1p(jnp.exp(-jnp.abs(z)))
    a = dt_ref[...] * -jnp.exp(par[0:1, :])
    r = lax.broadcasted_iota(jnp.int32, (length, length), 0)
    c = lax.broadcasted_iota(jnp.int32, (length, length), 1)
    lower = jnp.where(r >= c, 1.0, 0.0).astype(BF16)
    hi, mid, lo = thirds(a)
    cum = (dot(lower, hi) + (dot(lower, mid) + dot(lower, lo))) * LOG2E
    cum_ref[...] = cum
    cumt = cum.T
    cumt_ref[...] = cumt
    ecum[...] = jnp.exp2(cum)
    ecumt[...] = jnp.exp2(cumt)
    tail[...] = jnp.exp2(cum[length - 1 : length] - cum)
    bb, cc = b_ref[...], c_ref[...]
    gt[...] = jnp.where(c >= r, dot(bb, cc, NT), 0.0)
    dg[...] = jnp.zeros(dg.shape, F32)
    for ref in (cole_ref, skip_ref, ends, gr_ref, ddt):
        ref[...] = jnp.zeros(ref.shape, F32)
    c2 = jnp.concatenate([cc, cc], 0)
    b2 = jnp.concatenate([bb, bb], 1)
    lanes = lax.broadcasted_iota(jnp.int32, (1, two), 1)
    masks_f = [jnp.where(lanes < width, 1.0, 0.0), jnp.where(lanes < width, 0.0, 1.0)]
    masks = [m.astype(BF16) for m in masks_f]

    def columns(j):
        return pl.ds(pl.multiple_of(j * two, two), two)

    pl.semaphore_wait(barrier, n - 1)

    def check_copy(i):
        z = lax.rem(zi + i, group)
        to = (lax.axis_index("gx"), lax.axis_index("gy"), z)
        return remote(check_hbm.at[z], start_ref.at[zi], check_send, check_recv, to)

    for i in range(1, group):
        check_copy(i).start()
    load_g.wait()

    def turned(j):
        return lax.rem(j + lax.div(me, per), pairs) if per <= n else j

    def send_blocks(j):
        for i in range(per):
            d = turned(j) * per + i

            @pl.when(d != me)
            def _():
                remote(
                    block_ref.at[d], got_ref.at[me], block_send, block_recv, place(d)
                ).start()

            @pl.when(d == me)
            def _():
                pltpu.make_async_copy(block_ref.at[d], got_ref.at[me], block_recv).start()

    def first(jj, _):
        j = turned(jj)
        weighted = g_ref[:, columns(j)].astype(F32) * pair_columns(ecum[...], j, width)
        hi, lo = halves(weighted)
        state = dot(jnp.concatenate([hi, lo], 0), c2, TN)
        for i in range(per):
            head = 2 * j + (i * rows) // width
            block_ref[j * per + i, 0:rows, :] = state[i * rows : (i + 1) * rows]
            decay = ecumt[pl.ds(head, 1), :][:, length - 1 : length]
            block_ref[j * per + i, rows : rows + 8, :] = jnp.broadcast_to(decay, (8, LANES))

        @pl.when(jj > 0)
        def _():
            send_blocks(jj - 1)

        return 0

    lax.fori_loop(0, pairs, first, 0)
    load_x.wait()
    send_blocks(pairs - 1)

    def inner(j, _):
        at = columns(j)
        xp, gp = x_ref[:, at], g_ref[:, at]
        gs = [gp * m for m in masks]
        overlap = jnp.sum(xp.astype(F32) * gp.astype(F32), 0, keepdims=True)
        parts = [[], []]
        for k in range(2):
            h = 2 * j + k
            cs, ds = column(cum_ref[...], h), column(dt_ref[...], h)
            ct = cumt_ref[pl.ds(h, 1), :]
            xk = xp * masks[k]
            skip_ref[pl.ds(h, 1), :] = overlap * masks_f[k]
            total = None
            for q in range(2):
                s0 = q * half
                rs, ts = slice(s0, s0 + half), slice(s0, length)
                dm = dot(xk[rs], gp[ts], NT)
                low = jnp.exp2(jnp.minimum(ct[:, ts] - cs[rs], 0.0))
                scores = gt[rs, ts]
                parts[q] += list(halves(low * scores))
                dl = dm * (low * ds[rs])
                dg[rs, ts] += dl
                part = jnp.sum(dl * scores, 0, keepdims=True)
                if q == 0:
                    total = part
                else:
                    total = jnp.concatenate([total[:, :half], total[:, half:] + part], 1)
            cole_ref[pl.ds(h, 1), :] = total
        for q in range(2):
            s0 = q * half
            rhs = jnp.concatenate([gs[0][s0:], gs[0][s0:], gs[1][s0:], gs[1][s0:]], 0)
            dxi_ref[s0 : s0 + half, at] = dot(jnp.concatenate(parts[q], 1), rhs)
        return 0

    lax.fori_loop(0, pairs, inner, 0)

    pltpu.make_async_copy(got_ref, got_ref, block_recv).wait()

    def hop(k, acc):
        at = n - 1 - k
        carry_ref[at] = acc
        part = got_ref[at]
        return part[0:rows] + part[rows : rows + 1] * acc

    lax.fori_loop(0, n, hop, jnp.zeros((rows, LANES), F32))
    mine = lax.div(me, per)

    def send_carry(i, _):
        d = other(i)
        remote(
            carry_ref.at[d], later_ref.at[me], carry_send, carry_recv.at[mine], place(d)
        ).start()
        return 0

    lax.fori_loop(1, n, send_carry, 0)
    pltpu.make_async_copy(carry_ref.at[me], later_ref.at[me], carry_recv.at[mine]).start()

    d = jnp.where(c >= r, dg[...], 0.0)
    bg_ref[...] = dot(jnp.concatenate(halves(d), 1), jnp.concatenate([cc, cc], 0))
    cg_ref[...] = dot(jnp.concatenate(halves(d.T), 1), jnp.concatenate([bb, bb], 0))

    own_check.wait()
    for i in range(1, group):
        check_copy(i).wait_send()
    arrived = start_ref.at[pl.ds(0, group - 1)]
    pltpu.make_async_copy(arrived, arrived, check_recv).wait()

    def entering(j):
        return jnp.concatenate(
            [start_ref[q, 2 * j + k] for k in range(2) for q in range(group)], 0
        )

    def read(j, cg):
        gp = g_ref[:, columns(j)].astype(F32)
        hp = entering(j)
        gr_ref[...] += head_sum(gp * dot(cc, hp, NT), j, width)
        hi, lo = halves(gp * pair_columns(ecum[...], j, width))
        return cg + dot(jnp.concatenate([hi, lo], 1), jnp.concatenate([hp, hp], 0))

    cg_ref[...] = lax.fori_loop(0, pairs, read, cg_ref[...])

    def last(jj, bg):
        j = lax.rem(mine + pairs - jj, pairs)
        at = columns(j)
        come = later_ref.at[pl.ds(j * per, per)]
        pltpu.make_async_copy(come, come, carry_recv.at[j]).wait()
        later = jnp.concatenate([later_ref[j * per + i] for i in range(per)], 0)
        xp, gp = x_ref[:, at].astype(F32), g_ref[:, at].astype(F32)
        hp = entering(j).astype(F32)
        lhi, llo = halves(later)
        u = dot(b2, jnp.concatenate([lhi, llo], 1), NT)
        tp, dtp = pair_columns(tail[...], j, width), pair_columns(dt_ref[...], j, width)
        skips = pair_columns(par_ref[...], j, width)[2:3]
        tu = tp * u
        v = dxi_ref[:, at] + tu
        ddt[...] += head_sum(xp * v, j, width)
        dx_ref[:, at] = (dtp * v + skips * gp).astype(BF16)
        dx_w = dtp * xp
        cross = later * hp
        out = jnp.sum(dx_w * tu, 0, keepdims=True)
        for k in range(2):
            h = 2 * j + k
            own = jnp.sum(cross[k * width : (k + 1) * width], 0, keepdims=True)
            decay = ecumt[pl.ds(h, 1), :][:, length - 1 : length]
            ends[pl.ds(h, 1), :] = own * decay + out * masks_f[k]
        whi, wlo = halves(tp * dx_w)
        return bg + dot(
            jnp.concatenate([whi, wlo, whi], 1), jnp.concatenate([lhi, lhi, llo], 0)
        )

    bg = lax.fori_loop(0, pairs, last, bg_ref[...])
    dt = dt_ref[...]
    dd = ddt[...]
    dcum = cole_ref[...].T + ecum[...] * gr_ref[...] - dt * dd
    upper = jnp.where(c >= r, 1.0, 0.0).astype(BF16)
    hi, mid, lo = thirds(dcum)
    da = dot(upper, hi) + (dot(upper, mid) + dot(upper, lo))
    da = da + jnp.sum(ends[...].T, 0, keepdims=True)
    rate = -jnp.exp(par[0:1])
    total = (dd + da * rate)[:, :heads]
    draw = total * jax.nn.sigmoid(raw_ref[...] + par[1:2, :heads])
    part_ref[...] = jnp.zeros(part_ref.shape, F32)
    part_ref[0:1, :] = jnp.sum(da * dt, 0, keepdims=True) * rate
    part_ref[1:2, :heads] = jnp.sum(draw, 0, keepdims=True)
    part_ref[2:3, :] = jnp.sum(skip_ref[...].T, 0, keepdims=True)
    store = pltpu.make_async_copy(dx_ref, dx_hbm, store_sem)
    store.start()
    draw_ref[...] = draw
    bg_ref[...] = bg

    def send_part(i, _):
        remote(part_ref, parts_ref.at[me], part_send, part_recv, place(other(i))).start()
        return 0

    lax.fori_loop(1, n, send_part, 0)
    pltpu.make_async_copy(part_ref, parts_ref.at[me], part_recv).start()
    sent = block_ref.at[pl.ds(0, n - 1)]
    pltpu.make_async_copy(sent, sent, block_send).wait()
    sent = carry_ref.at[pl.ds(0, n - 1)]
    pltpu.make_async_copy(sent, sent, carry_send).wait()
    pltpu.make_async_copy(parts_ref, parts_ref, part_recv).wait()
    sum_ref[...] = lax.fori_loop(
        0, n, lambda i, acc: acc + parts_ref[i], jnp.zeros(sum_ref.shape, F32)
    )
    sent = parts_ref.at[pl.ds(0, n - 1)]
    pltpu.make_async_copy(sent, sent, part_send).wait()
    store.wait()


def local(sizes, x, raw, b_mat, c_mat, decay_log, bias, skip, checkpoints, grad):
    n = math.prod(sizes)
    length, heads = raw.shape
    wide = x.shape[1]
    width = wide // heads
    rows = wide // n
    assert b_mat.shape[1] == LANES and 2 * width == LANES and width % rows == 0
    assert heads <= LANES and sizes[2] == checkpoints.shape[0]
    par = jnp.pad(jnp.stack([decay_log, bias, skip]), ((0, 5), (0, LANES - heads)))
    tok, tok_t, square = (length, LANES), (LANES, length), (LANES, LANES)
    pairs = heads // 2
    vmem = [
        ((length, wide), BF16), ((length, wide), BF16), ((length, wide), BF16),
        (checkpoints.shape, BF16),
        ((n, rows + 8, LANES), F32), ((n, rows + 8, LANES), F32),
        ((n, rows, LANES), F32), ((n, rows, LANES), F32),
        (tok, F32), (tok, F32), (tok, F32), (tok, F32), (tok, F32), (tok, F32),
        (tok_t, F32), (tok_t, F32), (tok_t, F32), (square, F32), (square, F32),
        ((length, length), F32), ((length, length), F32), ((length, wide), F32),
        ((8, LANES), F32), ((n, 8, LANES), F32),
    ]
    dma = pltpu.SemaphoreType.DMA
    near = pl.BlockSpec(memory_space=pltpu.VMEM)
    far = pl.BlockSpec(memory_space=pltpu.HBM)
    outs = [
        ((length, wide), BF16), ((length, heads), F32), (tok, F32), (tok, F32),
        ((8, LANES), F32),
    ]
    dx, draw, bg, cg, total = pl.pallas_call(
        functools.partial(everything, n, sizes),
        out_shape=[jax.ShapeDtypeStruct(s, d) for s, d in outs],
        in_specs=[near] * 4 + [far] * 3,
        out_specs=[far] + [near] * 4,
        scratch_shapes=[pltpu.VMEM(s, d) for s, d in vmem]
        + [dma((3,)), dma(()), dma(()), dma(()), dma(()), dma(()), dma(()), dma((pairs,)),
           dma(()), dma(())],
        compiler_params=pltpu.CompilerParams(
            collective_id=0, has_side_effects=True, vmem_limit_bytes=56 * 1024 * 1024
        ),
        cost_estimate=pl.CostEstimate(
            flops=80 * length * wide * LANES, bytes_accessed=4 * length * wide, transcendentals=0
        ),
    )(raw, par, b_mat, c_mat, x, grad, checkpoints)
    return dx, draw, bg, cg, total[0, :heads], total[1, :heads], total[2, :heads]


def solution(mesh):
    tokens = P(AXES, None)
    sizes = tuple(mesh.shape[a] for a in AXES)
    return jax.shard_map(
        functools.partial(local, sizes),
        mesh=mesh,
        in_specs=(tokens,) * 4 + (P(),) * 3 + (P(("gx", "gy"), None, "gz", None), tokens),
        out_specs=(tokens,) * 4 + (P(),) * 3,
        check_vma=False,
    )
```

time: 153 us -> 90.7 us (0.59)
  blocking collectives: 76.7 us -> 0 us
  Pallas kernels: 35.8 us -> 80 us
  waiting for transfers between devices: 21 us -> 0 us
  starting transfers between devices: 6.12 us -> 0 us
  local copies, waits for them, and re-layouts: 11 us -> 9.05 us
    pallas_call x5 -> x1, Pallas kernels: 35.8 us -> 80 us  [local(): pl.pallas_call(functools.partial(everything, n, sizes), out_shape=[jax.Sh...]
    psum x1 -> x0, blocking collectives: 38.9 us -> none  [local(): total = lax.psum(part, AXES)]
    all_to_all x1 -> x0, blocking collectives: 37.8 us -> none  [local(): got = lax.all_to_all(blocks, AXES, split_axis=0, concat_axis=0, tiled=True)]
    all_to_all x2 -> x0, waiting for transfers between devices: 21 us -> none  [the longest x1 13.8 us: local(): lax.all_to_all(checkpoints, 'gz', split_axis=0, concat_axis=2, tiled=True)]
    all_to_all x2 -> x0, starting transfers between devices: 6.12 us -> none  [the longest x1 3.47 us: local(): lax.all_to_all(checkpoints, 'gz', split_axis=0, concat_axis=2, tiled=True)]
    unnamed x28 -> x15, local copies, waits for them, and re-layouts: 10.4 us -> 7.74 us
  transfers between devices with their start and end apart: 2 -> 0, of which waited for: 2 -> 0; matrix products, arithmetic and copies ran while one was open for 0% -> 0% of each run, Pallas kernels for 12% -> 0%
where the time goes in v2:
time: 90.7 us; the launch traced here: 90.3 us
  Pallas kernels  80 us (88%)
  local copies, waits for them, and re-layouts  9.05 us (10%)
    pallas_call x1, Pallas kernels, local(): pl.pallas_call(functools.partial(everything, n, sizes), out_shape=[jax.Sh...  80 us
    unnamed x15, local copies, waits for them, and re-layouts  7.74 us

profile of v2, /device:TPU:0, one launch (start us, length us, event | category | flops | bytes accessed | tf_op | source)
XLA Modules:
  0.0 90.3 jit_solution(18268134753461262868)
XLA Ops:
  0.6 1.5 %copy.16.raw_ref = f32[256,32]{1,0:T(8,128)} copy(f32[256,32]{0,1:T(8,128)} %param.10) | data formatting | bytes 65536 | tf_op args[1]
  2.1 0.0 copy-start.2
  2.1 0.0 copy-start.3
  2.1 0.0 copy-start.4
  2.2 0.6 copy-done.2
  2.8 0.0 copy-done.3
  2.8 0.0 copy-done.4
  2.8 0.6 select_maximum_fusion.par_ref
  3.4 80.0 %shard_map.144 = (bf16[256,2048]{1,0:T(8,128)(2,1)}, f32[256,32]{1,0:T(8,128)}, f32[256,128]{1,0:T(8,128)}, f32[256,128]{1,0:T(8,128)}, f32[8,128]{1,0:T(8,128)}) custom-call(f32[256,32]{1,0:T(8,128)} %copy.16.raw_ref, f32[8,128]{1,0:T(8,128)} %select_maximum_fusion.par_ref, bf16[256,128]{1,0:T(8,128)(2,1)} %b_ref.1, bf16[256,128]{1,0:T(8,128)(2,1)} %c_ref.1, ...), custom_call_target="tpu_custom_call" | custom-call | flops 5368709120 | bytes 2097152 | tf_op jit(solution)/shard_map/pallas_call | solution.py:367
  83.5 1.3 %slice_bitcast_fusion = (f32[32]{0:T(128)}, f32[32]{0:T(128)}, f32[32]{0:T(128)}) fusion(f32[8,128]{1,0:T(8,128)} %get-tuple-element.16), kind=kLoop, calls=%fused_computation.4 | loop fusion | bytes 768 | tf_op jit(solution)/shard_map/squeeze | solution.py:382
  84.8 1.6 %copy.17 = f32[256,32]{0,1:T(8,128)} copy(f32[256,32]{1,0:T(8,128)} %get-tuple-element.18) | data formatting | bytes 65536
  86.4 0.0 copy-start.1
  86.4 2.3 %copy.21 = bf16[256,2048]{1,0:T(8,128)(2,1)} copy(bf16[256,2048]{1,0:T(8,128)(2,1)} %get-tuple-element.34) | data formatting | bytes 2097152
  88.7 0.0 copy-done.1
  88.7 0.0 copy-start
  88.7 0.7 copy.22
  89.4 0.3 copy-done
  89.7 0.7 copy.23
Async XLA Ops:
  2.1 0.7 copy-start.2
  2.1 0.7 copy-start.3
  2.1 0.7 copy-start.4
  86.4 2.3 %copy-start.1 = (f32[256,128]{1,0:T(8,128)S(1)}, f32[256,128]{1,0:T(8,128)}, u32[]{:S(2)}) copy-start(f32[256,128]{1,0:T(8,128)} %get-tuple-element.36) | copy-start | bytes 393220
  88.7 1.0 %copy-start = (f32[256,128]{1,0:T(8,128)S(1)}, f32[256,128]{1,0:T(8,128)}, u32[]{:S(2)}) copy-start(f32[256,128]{1,0:T(8,128)} %get-tuple-element.37) | copy-start | bytes 393220

commit v3 on v2

--- a/solution.py
+++ b/solution.py
@@ -55,15 +55,15 @@
 
 
 def everything(
-    n, sizes, raw_ref, par_ref, b_ref, c_ref, x_hbm, g_hbm, check_hbm,
-    dx_hbm, draw_ref, bg_ref, cg_ref, sum_ref,
+    n, sizes, rawt_ref, decay_ref, bias_ref, gain_ref, b_ref, c_ref, x_hbm, g_hbm, check_hbm,
+    dx_hbm, drawt_ref, bg_ref, cg_ref, sum_ref,
     x_ref, g_ref, dx_ref, start_ref, block_ref, got_ref, carry_ref, later_ref,
     cum_ref, dt_ref, ecum, tail, gr_ref, ddt, cumt_ref, ecumt, cole_ref, skip_ref, ends,
-    gt, dg, dxi_ref, part_ref, parts_ref,
-    load_sem, store_sem, check_send, check_recv, block_send, block_recv,
+    gt, dg, dxi_ref, part_ref, parts_ref, par_ref, row_ref, rows_ref, rates_ref,
+    load_sem, store_sem, row_send, row_recv, check_send, check_recv, block_send, block_recv,
     carry_send, carry_recv, part_send, part_recv,
 ):
-    length, heads = raw_ref.shape
+    heads, length = rawt_ref.shape
     wide = x_ref.shape[1]
     width = wide // heads
     two = 2 * width
@@ -108,10 +108,14 @@
 
     lax.fori_loop(1, n, greet, 0)
 
+    par_ref[...] = jnp.zeros(par_ref.shape, F32)
+    for at, ref in enumerate((decay_ref, bias_ref, gain_ref)):
+        par_ref[at : at + 1, :heads] = ref[...]
     par = par_ref[...]
-    dt_ref[...] = jnp.zeros(dt_ref.shape, F32)
-    z = raw_ref[...] + par[1:2, :heads]
-    dt_ref[:, :heads] = jnp.maximum(z, 0.0) + jnp.log1p(jnp.exp(-jnp.abs(z)))
+    cumt_ref[...] = jnp.zeros(cumt_ref.shape, F32)
+    cumt_ref[:heads, :] = rawt_ref[...]
+    z = cumt_ref[...].T + par[1:2]
+    dt_ref[...] = jnp.maximum(z, 0.0) + jnp.log1p(jnp.exp(-jnp.abs(z)))
     a = dt_ref[...] * -jnp.exp(par[0:1, :])
     r = lax.broadcasted_iota(jnp.int32, (length, length), 0)
     c = lax.broadcasted_iota(jnp.int32, (length, length), 1)
@@ -122,6 +126,7 @@
     cumt = cum.T
     cumt_ref[...] = cumt
     ecum[...] = jnp.exp2(cum)
+    row_ref[...] = jnp.exp2(cum[length - 1 : length])
     ecumt[...] = jnp.exp2(cumt)
     tail[...] = jnp.exp2(cum[length - 1 : length] - cum)
     bb, cc = b_ref[...], c_ref[...]
@@ -145,9 +150,14 @@
         to = (lax.axis_index("gx"), lax.axis_index("gy"), z)
         return remote(check_hbm.at[z], start_ref.at[zi], check_send, check_recv, to)
 
-    for i in range(1, group):
-        check_copy(i).start()
     load_g.wait()
+
+    def send_row(i, _):
+        remote(row_ref, rows_ref.at[me], row_send, row_recv, place(other(i))).start()
+        return 0
+
+    lax.fori_loop(1, n, send_row, 0)
+    pltpu.make_async_copy(row_ref, rows_ref.at[me], row_recv).start()
 
     def turned(j):
         return lax.rem(j + lax.div(me, per), pairs) if per <= n else j
@@ -172,10 +182,7 @@
         hi, lo = halves(weighted)
         state = dot(jnp.concatenate([hi, lo], 0), c2, TN)
         for i in range(per):
-            head = 2 * j + (i * rows) // width
-            block_ref[j * per + i, 0:rows, :] = state[i * rows : (i + 1) * rows]
-            decay = ecumt[pl.ds(head, 1), :][:, length - 1 : length]
-            block_ref[j * per + i, rows : rows + 8, :] = jnp.broadcast_to(decay, (8, LANES))
+            block_ref[j * per + i] = state[i * rows : (i + 1) * rows]
 
         @pl.when(jj > 0)
         def _():
@@ -186,6 +193,8 @@
     lax.fori_loop(0, pairs, first, 0)
     load_x.wait()
     send_blocks(pairs - 1)
+    for i in range(1, group):
+        check_copy(i).start()
 
     def inner(j, _):
         at = columns(j)
@@ -223,13 +232,22 @@
 
     lax.fori_loop(0, pairs, inner, 0)
 
+    pltpu.make_async_copy(rows_ref, rows_ref, row_recv).wait()
+    head = lax.div(me * rows, width)
+    pick = jnp.where(lax.broadcasted_iota(jnp.int32, (1, LANES), 1) == head, 1.0, 0.0)
+
+    def rate_of(i, _):
+        rate = jnp.sum(rows_ref[i] * pick, 1, keepdims=True)
+        rates_ref[i] = jnp.broadcast_to(rate, (1, LANES))
+        return 0
+
+    lax.fori_loop(0, n, rate_of, 0)
     pltpu.make_async_copy(got_ref, got_ref, block_recv).wait()
 
     def hop(k, acc):
         at = n - 1 - k
         carry_ref[at] = acc
-        part = got_ref[at]
-        return part[0:rows] + part[rows : rows + 1] * acc
+        return got_ref[at] + rates_ref[at] * acc
 
     lax.fori_loop(0, n, hop, jnp.zeros((rows, LANES), F32))
     mine = lax.div(me, per)
@@ -298,6 +316,8 @@
         )
 
     bg = lax.fori_loop(0, pairs, last, bg_ref[...])
+    store = pltpu.make_async_copy(dx_ref, dx_hbm, store_sem)
+    store.start()
     dt = dt_ref[...]
     dd = ddt[...]
     dcum = cole_ref[...].T + ecum[...] * gr_ref[...] - dt * dd
@@ -306,15 +326,13 @@
     da = dot(upper, hi) + (dot(upper, mid) + dot(upper, lo))
     da = da + jnp.sum(ends[...].T, 0, keepdims=True)
     rate = -jnp.exp(par[0:1])
-    total = (dd + da * rate)[:, :heads]
-    draw = total * jax.nn.sigmoid(raw_ref[...] + par[1:2, :heads])
+    cumt_ref[:heads, :] = rawt_ref[...]
+    draw = (dd + da * rate) * jax.nn.sigmoid(cumt_ref[...].T + par[1:2])
     part_ref[...] = jnp.zeros(part_ref.shape, F32)
     part_ref[0:1, :] = jnp.sum(da * dt, 0, keepdims=True) * rate
-    part_ref[1:2, :heads] = jnp.sum(draw, 0, keepdims=True)
+    part_ref[1:2, :] = jnp.sum(draw, 0, keepdims=True)
     part_ref[2:3, :] = jnp.sum(skip_ref[...].T, 0, keepdims=True)
-    store = pltpu.make_async_copy(dx_ref, dx_hbm, store_sem)
-    store.start()
-    draw_ref[...] = draw
+    drawt_ref[...] = draw.T[:heads]
     bg_ref[...] = bg
 
     def send_part(i, _):
@@ -333,6 +351,8 @@
     )
     sent = parts_ref.at[pl.ds(0, n - 1)]
     pltpu.make_async_copy(sent, sent, part_send).wait()
+    sent = rows_ref.at[pl.ds(0, n - 1)]
+    pltpu.make_async_copy(sent, sent, row_send).wait()
     store.wait()
 
 
@@ -344,33 +364,33 @@
     rows = wide // n
     assert b_mat.shape[1] == LANES and 2 * width == LANES and width % rows == 0
     assert heads <= LANES and sizes[2] == checkpoints.shape[0]
-    par = jnp.pad(jnp.stack([decay_log, bias, skip]), ((0, 5), (0, LANES - heads)))
     tok, tok_t, square = (length, LANES), (LANES, length), (LANES, LANES)
     pairs = heads // 2
     vmem = [
         ((length, wide), BF16), ((length, wide), BF16), ((length, wide), BF16),
         (checkpoints.shape, BF16),
-        ((n, rows + 8, LANES), F32), ((n, rows + 8, LANES), F32),
+        ((n, rows, LANES), F32), ((n, rows, LANES), F32),
         ((n, rows, LANES), F32), ((n, rows, LANES), F32),
         (tok, F32), (tok, F32), (tok, F32), (tok, F32), (tok, F32), (tok, F32),
         (tok_t, F32), (tok_t, F32), (tok_t, F32), (square, F32), (square, F32),
         ((length, length), F32), ((length, length), F32), ((length, wide), F32),
-        ((8, LANES), F32), ((n, 8, LANES), F32),
+        ((8, LANES), F32), ((n, 8, LANES), F32), ((8, LANES), F32),
+        ((1, LANES), F32), ((n, 1, LANES), F32), ((n, 1, LANES), F32),
     ]
     dma = pltpu.SemaphoreType.DMA
     near = pl.BlockSpec(memory_space=pltpu.VMEM)
     far = pl.BlockSpec(memory_space=pltpu.HBM)
     outs = [
-        ((length, wide), BF16), ((length, heads), F32), (tok, F32), (tok, F32),
+        ((length, wide), BF16), ((heads, length), F32), (tok, F32), (tok, F32),
         ((8, LANES), F32),
     ]
     dx, draw, bg, cg, total = pl.pallas_call(
         functools.partial(everything, n, sizes),
         out_shape=[jax.ShapeDtypeStruct(s, d) for s, d in outs],
-        in_specs=[near] * 4 + [far] * 3,
+        in_specs=[near] * 6 + [far] * 3,
         out_specs=[far] + [near] * 4,
         scratch_shapes=[pltpu.VMEM(s, d) for s, d in vmem]
-        + [dma((3,)), dma(()), dma(()), dma(()), dma(()), dma(()), dma(()), dma((pairs,)),
+        + [dma((3,)), dma(()), dma(()), dma(()), dma(()), dma(()), dma(()), dma(()), dma(()), dma((pairs,)),
            dma(()), dma(())],
         compiler_params=pltpu.CompilerParams(
             collective_id=0, has_side_effects=True, vmem_limit_bytes=56 * 1024 * 1024
@@ -378,8 +398,8 @@
         cost_estimate=pl.CostEstimate(
             flops=80 * length * wide * LANES, bytes_accessed=4 * length * wide, transcendentals=0
         ),
-    )(raw, par, b_mat, c_mat, x, grad, checkpoints)
-    return dx, draw, bg, cg, total[0, :heads], total[1, :heads], total[2, :heads]
+    )(raw.T, decay_log[None], bias[None], skip[None], b_mat, c_mat, x, grad, checkpoints)
+    return dx, draw.T, bg, cg, total[0, :heads], total[1, :heads], total[2, :heads]
 
 
 def solution(mesh):

time: 90.7 us -> 82.4 us (0.908)
  Pallas kernels: 80 us -> 75.6 us
  local copies, waits for them, and re-layouts: 9.05 us -> 5.87 us
    pallas_call x1, Pallas kernels: 80 us -> 75.6 us  [local(): pl.pallas_call(functools.partial(everything, n, sizes), out_shape=[jax.Sh...]
    unnamed x15 -> x10, local copies, waits for them, and re-layouts: 7.74 us -> 4.57 us
where the time goes in v3:
time: 82.4 us; the launch traced here: 82.1 us
  Pallas kernels  75.6 us (92%)
  local copies, waits for them, and re-layouts  5.87 us (7%)
    pallas_call x1, Pallas kernels, local(): pl.pallas_call(functools.partial(everything, n, sizes), out_shape=[jax.Sh...  75.6 us
    unnamed x10, local copies, waits for them, and re-layouts  4.57 us

profile of v3, /device:TPU:0, one launch (start us, length us, event | category | flops | bytes accessed | tf_op | source)
XLA Modules:
  0.0 82.1 jit_solution(12988789741816730049)
XLA Ops:
  0.6 75.6 %shard_map.144 = (bf16[256,2048]{1,0:T(8,128)(2,1)}, f32[32,256]{1,0:T(8,128)}, f32[256,128]{1,0:T(8,128)}, f32[256,128]{1,0:T(8,128)}, f32[8,128]{1,0:T(8,128)}) custom-call(f32[32,256]{1,0:T(8,128)} %bitcast.12, f32[1,32]{1,0:T(1,128)} %bitcast.13, f32[1,32]{1,0:T(1,128)} %bitcast.14, f32[1,32]{1,0:T(1,128)} %bitcast.15, bf16[256,128]{1,0:T(8,128)(2,1)} %b_ref.1, ...), custom_call_target="tpu_custom_call" | custom-call | flops 5368709120 | bytes 2097152 | tf_op jit(solution)/shard_map/pallas_call | solution.py:387
  76.3 1.3 %slice_bitcast_fusion = (f32[32]{0:T(128)}, f32[32]{0:T(128)}, f32[32]{0:T(128)}) fusion(f32[8,128]{1,0:T(8,128)} %get-tuple-element.16), kind=kLoop, calls=%fused_computation | loop fusion | bytes 768 | tf_op jit(solution)/shard_map/squeeze | solution.py:402
  77.6 0.0 copy-start.2
  77.6 0.0 copy-start.1
  77.6 2.3 %copy.20 = bf16[256,2048]{1,0:T(8,128)(2,1)} copy(bf16[256,2048]{1,0:T(8,128)(2,1)} %get-tuple-element.27) | data formatting | bytes 2097152
  79.9 0.0 copy-done.2
  79.9 0.6 copy.21
  80.5 0.0 copy-done.1
  80.5 0.0 copy-start
  80.5 0.7 copy.22
  81.2 0.3 copy-done
  81.5 0.7 copy.23
Async XLA Ops:
  77.6 2.3 %copy-start.2 = (f32[32,256]{1,0:T(8,128)S(1)}, f32[32,256]{1,0:T(8,128)}, u32[]{:S(2)}) copy-start(f32[32,256]{1,0:T(8,128)} %get-tuple-element.13) | copy-start | bytes 98308
  77.6 3.0 %copy-start.1 = (f32[256,128]{1,0:T(8,128)S(1)}, f32[256,128]{1,0:T(8,128)}, u32[]{:S(2)}) copy-start(f32[256,128]{1,0:T(8,128)} %get-tuple-element.29) | copy-start | bytes 393220
  80.5 1.0 %copy-start = (f32[256,128]{1,0:T(8,128)S(1)}, f32[256,128]{1,0:T(8,128)}, u32[]{:S(2)}) copy-start(f32[256,128]{1,0:T(8,128)} %get-tuple-element.30) | copy-start | bytes 393220

commit v4 on v3

--- a/solution.py
+++ b/solution.py
@@ -354,6 +354,20 @@
     sent = rows_ref.at[pl.ds(0, n - 1)]
     pltpu.make_async_copy(sent, sent, row_send).wait()
     store.wait()
+
+
+def hand_over(
+    dx_in, draw_in, bg_in, cg_in, sum_in, dx_ref, draw_ref, bg_ref, cg_ref, *sum_refs
+):
+    dx_ref[...] = dx_in[...]
+
+    @pl.when(pl.program_id(0) == 0)
+    def _():
+        draw_ref[...] = draw_in[...]
+        bg_ref[...] = bg_in[...]
+        cg_ref[...] = cg_in[...]
+        for at, ref in enumerate(sum_refs):
+            ref[...] = sum_in[at : at + 1, : ref.shape[1]]
 
 
 def local(sizes, x, raw, b_mat, c_mat, decay_log, bias, skip, checkpoints, grad):
@@ -399,7 +413,23 @@
             flops=80 * length * wide * LANES, bytes_accessed=4 * length * wide, transcendentals=0
         ),
     )(raw.T, decay_log[None], bias[None], skip[None], b_mat, c_mat, x, grad, checkpoints)
-    return dx, draw.T, bg, cg, total[0, :heads], total[1, :heads], total[2, :heads]
+    steps = 4
+
+    def whole(shape):
+        return pl.BlockSpec(shape, lambda i: (0, 0))
+
+    moved = pl.BlockSpec((length // steps, wide), lambda i: (i, 0))
+    small = [whole((heads, length)), whole(tok), whole(tok)]
+    one = (1, heads)
+    dx, draw, bg, cg, *sums = pl.pallas_call(
+        hand_over,
+        grid=(steps,),
+        out_shape=[jax.ShapeDtypeStruct(s, d) for s, d in outs[:4] + [(one, F32)] * 3],
+        in_specs=[moved] + small + [whole((8, LANES))],
+        out_specs=[moved] + small + [whole(one)] * 3,
+        compiler_params=pltpu.CompilerParams(vmem_limit_bytes=56 * 1024 * 1024),
+    )(dx, draw, bg, cg, total)
+    return (dx, draw.T, bg, cg, *(part[0] for part in sums))
 
 
 def solution(mesh):

time: 82.4 us -> 80.1 us (0.972)
  local copies, waits for them, and re-layouts: 5.87 us -> 0 us
  Pallas kernels: 75.6 us -> 79.2 us
    unnamed x10 -> x0, local copies, waits for them, and re-layouts: 4.57 us -> none
    pallas_call x0 -> x1, Pallas kernels: none -> 3.63 us  [local(): pl.pallas_call(hand_over, grid=(steps,), out_shape=[jax.ShapeDtypeStruct(...]
    squeeze x1 -> x0, local copies, waits for them, and re-layouts: 1.31 us -> none  [local(): total[2, :heads]]
where the time goes in v4:
time: 80.1 us; the launch traced here: 79.9 us
  Pallas kernels  79.2 us (99%)
    pallas_call x1, Pallas kernels, local(): pl.pallas_call(functools.partial(everything, n, sizes), out_shape=[jax.Sh...  75.6 us
    pallas_call x1, Pallas kernels, local(): pl.pallas_call(hand_over, grid=(steps,), out_shape=[jax.ShapeDtypeStruct(...  3.63 us

profile of v4, /device:TPU:0, one launch (start us, length us, event | category | flops | bytes accessed | tf_op | source)
XLA Modules:
  0.0 79.9 jit_solution(745156589882632731)
XLA Ops:
  0.6 75.6 %shard_map.144 = (bf16[256,2048]{1,0:T(8,128)(2,1)}, f32[32,256]{1,0:T(8,128)}, f32[256,128]{1,0:T(8,128)}, f32[256,128]{1,0:T(8,128)}, f32[8,128]{1,0:T(8,128)}) custom-call(f32[32,256]{1,0:T(8,128)} %bitcast.8, f32[1,32]{1,0:T(1,128)} %bitcast.10, f32[1,32]{1,0:T(1,128)} %bitcast.11, f32[1,32]{1,0:T(1,128)} %bitcast.12, bf16[256,128]{1,0:T(8,128)(2,1)} %b_ref.1, ...), custom_call_target="tpu_custom_call" | custom-call | flops 5368709120 | bytes 2097152 | tf_op jit(solution)/shard_map/pallas_call | solution.py:401
  76.3 3.6 %shard_map.145 = (bf16[256,2048]{1,0:T(8,128)(2,1)}, f32[32,256]{1,0:T(8,128)}, f32[256,128]{1,0:T(8,128)}, f32[256,128]{1,0:T(8,128)}, f32[1,32]{1,0:T(1,128)}, /*index=5*/f32[1,32]{1,0:T(1,128)}, f32[1,32]{1,0:T(1,128)}) custom-call(bf16[256,2048]{1,0:T(8,128)(2,1)} %get-tuple-element.19.dx_in, f32[32,256]{1,0:T(8,128)} %get-tuple-element.20.draw_in, ...), custom_call_target="tpu_custom_call" | custom-call | tf_op jit(solution)/shard_map/pallas_call | solution.py:424
